TPU v7x, 256 devices: a whole 4x4x8 slice. The times are simulated.
256 devices in a mesh: expert: 64 (over y, z, core), token: 4 (over x).
Axes of the slice: x: 4, y: 4, z: 8, core: 2. Of those that a mesh axis runs over, the one named last changes fastest.
Arguments:
- cotangent: bfloat16 [32768, 2048], P(('expert', 'token')), may hold values from -6 to 6
- expert_ids: int32 [32768, 6], P(('expert', 'token')), may hold values from 0 to 63, all different within a row; in each aligned block of 128 rows (0 to 127, 128 to 255, ...) at most 14 rows name the same one
- gate_values: float32 [32768, 6], P(('expert', 'token')), may hold values from 0.05 to 0.45
- hidden_pre: bfloat16 [64, 3584, 768], P('expert', 'token'), may hold values from -8 to 8
- up_weight: bfloat16 [64, 2048, 768], P('expert'), may hold values from -0.125 to 0.125
- down_weight: bfloat16 [64, 2048, 768], P('expert'), may hold values from -0.21875 to 0.21875
Outputs:
- input_grad: bfloat16 [32768, 2048], P(('expert', 'token'))
- down_grad: bfloat16 [64, 2048, 768], P('expert', 'token')
Inputs may be any that keep to these rules, and one draw needn't show every extreme that they name: `expert_ids`: each row names 6 different experts. Among the 128 rows of one device no expert is named more than 14 times, and in every draw some expert is named exactly 14 times by the rows of some device.
All inputs are finite; a program needn't handle non-finite values.
Results may differ from a plain program's by a relative error of at most 0.007.
Values may be sent and summed in bfloat16 or wider, within the bound.
A program may use at most 128 MiB of HBM per device.

v0:
```python
import jax
import jax.numpy as jnp
from jax import lax
from jax.sharding import PartitionSpec as P

grad_scale = 0.03125
root_half = 0.7071067811865476
inv_root_two_pi = 0.3989422804014327


def slope_and_act(hidden_rows):
    values = hidden_rows.astype(jnp.float32)
    normal_cdf = 0.5 * (1.0 + lax.erf(values * root_half))
    density = inv_root_two_pi * jnp.exp(-0.5 * values * values)
    slopes = normal_cdf + values * density
    active = (values * normal_cdf).astype(jnp.bfloat16)
    return (slopes, active)


def route_tables(expert_ids, experts, capacity):
    routes = expert_ids.reshape(-1)
    one_hot = (routes[:, None] == jnp.arange(experts, dtype=jnp.int32)[None, :]).astype(jnp.int32)
    earlier = jnp.cumsum(one_hot, axis=0) - one_hot
    rank_in = jnp.sum(earlier * one_hot, axis=1)
    target = routes * capacity + rank_in
    slot_match = target[None, :] == jnp.arange(experts * capacity, dtype=jnp.int32)[:, None]
    route_index = jnp.arange(routes.shape[0], dtype=jnp.int32)[None, :]
    route_of_slot = jnp.sum(jnp.where(slot_match, route_index, 0), axis=1)
    slot_live = jnp.any(slot_match, axis=1)
    return (target, route_of_slot, slot_live)


def dispatch(slot_rows, experts):
    shaped = slot_rows.reshape(experts, -1, slot_rows.shape[1])
    arrived = lax.all_to_all(shaped, "expert", split_axis=0, concat_axis=0, tiled=True)
    return arrived.reshape(slot_rows.shape)


def transpose_jacobian(token_rows, tables, slopes, up_weight, down_weight, gate_values, experts):
    target, route_of_slot, slot_live = tables
    top_count = gate_values.shape[1]
    picked = jnp.take(token_rows, route_of_slot // top_count, axis=0)
    picked = jnp.where(slot_live[:, None], picked, jnp.zeros_like(picked))
    arrived = dispatch(picked, experts)
    inner_prod = jnp.dot(arrived, down_weight, preferred_element_type=jnp.float32)
    scaled = (inner_prod * slopes).astype(jnp.bfloat16)
    pieces = lax.dot_general(
        scaled, up_weight, (((1,), (1,)), ((), ())), preferred_element_type=jnp.float32
    ).astype(jnp.bfloat16)
    shaped = pieces.reshape(experts, -1, pieces.shape[1])
    returned = lax.all_to_all(shaped, "expert", split_axis=0, concat_axis=0, tiled=True).reshape(
        pieces.shape
    )
    per_route = jnp.take(returned, target, axis=0).astype(jnp.float32)
    per_route = per_route.reshape(gate_values.shape[0], top_count, -1)
    combined = jnp.sum(per_route * gate_values[:, :, None], axis=1)
    return combined.astype(jnp.bfloat16)


def body(cotangent, expert_ids, gate_values, hidden_pre, up_weight, down_weight):
    experts = lax.axis_size("expert")
    slopes, active = slope_and_act(hidden_pre[0])
    capacity = slopes.shape[0] // experts
    tables = route_tables(expert_ids, experts, capacity)
    first_term = transpose_jacobian(
        cotangent, tables, slopes, up_weight[0], down_weight[0], gate_values, experts
    )
    second = transpose_jacobian(
        first_term, tables, slopes, up_weight[0], down_weight[0], gate_values, experts
    )
    input_grad = (
        cotangent.astype(jnp.float32) + first_term.astype(jnp.float32) + second.astype(jnp.float32)
    ).astype(jnp.bfloat16)
    target, route_of_slot, slot_live = tables
    top_count = gate_values.shape[1]
    slot_gate = jnp.where(slot_live, jnp.take(gate_values.reshape(-1), route_of_slot), 0.0)
    picked = jnp.take(input_grad, route_of_slot // top_count, axis=0).astype(jnp.float32)
    routed = (picked * slot_gate[:, None]).astype(jnp.bfloat16)
    arrived = dispatch(routed, experts)
    grad_parts = lax.all_to_all(arrived, "token", split_axis=1, concat_axis=0, tiled=True)
    summed = lax.dot_general(
        grad_parts,
        lax.all_gather(active, "token", axis=0, tiled=True),
        (((0,), (0,)), ((), ())),
        preferred_element_type=jnp.float32,
    )
    grad_out = (summed * grad_scale).astype(jnp.bfloat16)[None]
    return (input_grad, grad_out)


def solution(mesh):
    in_specs = (
        P(("expert", "token"), None),
        P(("expert", "token"), None),
        P(("expert", "token"), None),
        P("expert", "token", None),
        P("expert", None, None),
        P("expert", None, None),
    )
    out_specs = (P(("expert", "token"), None), P("expert", "token", None))
    return jax.shard_map(body, mesh=mesh, in_specs=in_specs, out_specs=out_specs, check_vma=False)
```

profile of v0, /device:TPU:7, one launch (start us, length us, event | category | flops | bytes accessed | tf_op | source)
XLA Modules:
  0.0 771.9 jit_solution(15117301412643574991)
XLA Ops:
  7.2 0.0 copy-start
  7.2 0.9 copy.21
  8.1 0.1 eq.39
  8.3 0.1 reshape.122
  8.4 1.8 reduce-window.6
  10.2 0.3 slice_reduce_fusion
  10.5 0.1 fusion.25
  10.7 0.4 select_reduce_fusion
  11.0 0.4 fusion.13
  11.5 9.9 %gather_fusion.1 = bf16[896,2048]{1,0:T(8,128)(2,1)} fusion(bf16[128,2048]{1,0:T(8,128)(2,1)} %param.10, s32[1024]{0:T(1024)S(1)} %pad_clamp_fusion.2), kind=kCustom, calls=%fused_computation.clone | custom fusion | bytes 7343616 | tf_op jit(solution)/shard_map/jit(_take)/gather | solution.py:42
  21.3 3.8 select_select_fusion.1
  25.1 6.0 reshape.124
  31.1 108.6 %all_to_all.44 = bf16[64,14,2048]{2,1,0:T(8,128)(2,1)} all-to-all(bf16[64,14,2048]{2,1,0:T(8,128)(2,1)} %reshape.124), channel_id=1, replica_groups=mesh['expert'=64,'token'=4] {'expert'}, dimensions={0} | all-to-all | bytes 7340032 | tf_op jit(solution)/shard_map/all_to_all | solution.py:35
  139.7 6.0 reshape.125
  145.7 0.0 copy-done
  145.7 11.0 %convolution_convert_fusion.1 = bf16[896,2048]{1,0:T(8,128)(2,1)} fusion(bf16[1,2048,768]{2,1,0:T(8,128)(2,1)S(1)} %copy-done, bf16[896,2048]{1,0:T(8,128)(2,1)} %reshape.125, bf16[1,2048,768]{2,1,0:T(8,128)(2,1)} %param.15, bf16[1,896,768]{2,1,0:T(8,128)(2,1)} %param.13), kind=kOutput, calls=%fused_computation.17 | convolution fusion | flops 5646548992 | bytes 15007744 | tf_op jit(solution)/shard_map/dot_general | solution.py:47
  156.6 6.0 reshape.126
  162.6 0.0 copy-start.6
  162.6 6.5 all-to-all-start.1
  169.2 0.0 copy-done.6
  169.2 0.1 copy.24
  169.3 95.5 %all-to-all-done.1 = bf16[64,14,2048]{2,1,0:T(8,128)(2,1)} async-done(((bf16[64,14,2048]{2,1,0:T(8,128)(2,1)}), bf16[64,14,2048]{2,1,0:T(8,128)(2,1)}, u32[]{:S(2)}, u32[]{:S(2)}) %all-to-all-start.1) | async-done | bytes 3670048 | tf_op jit(solution)/shard_map/all_to_all | solution.py:51
  264.8 6.0 reshape.127
  270.8 9.6 %gather_fusion.2 = bf16[768,2048]{1,0:T(8,128)(2,1)} fusion(bf16[896,2048]{1,0:T(8,128)(2,1)} %reshape.127, s32[1024]{0:T(1024)S(1)} %pad_clamp_fusion.1), kind=kCustom, calls=%fused_computation.1.clone | custom fusion | bytes 6294528 | tf_op jit(solution)/shard_map/jit(_take)/gather | solution.py:54
  280.4 5.1 select_convert_fusion.1
  285.5 7.8 %reshape.140 = f32[128,6,2048]{2,1,0:T(8,128)} reshape(f32[768,2048]{1,0:T(8,128)} %select_convert_fusion.1) | data formatting | bytes 12582912 | tf_op jit(solution)/shard_map/reshape | solution.py:55
  293.3 7.4 multiply_reduce_fusion.1
  300.7 9.9 %gather_fusion.3 = bf16[896,2048]{1,0:T(8,128)(2,1)} fusion(bf16[128,2048]{1,0:T(8,128)(2,1)} %multiply_reduce_fusion.1, s32[1024]{0:T(1024)S(1)} %pad_clamp_fusion.2), kind=kCustom, calls=%fused_computation.2.clone | custom fusion | bytes 7343616 | tf_op jit(solution)/shard_map/jit(_take)/gather | solution.py:42
  310.6 3.8 select_select_fusion
  314.3 6.0 reshape.130
  320.3 102.3 %all_to_all.45 = bf16[64,14,2048]{2,1,0:T(8,128)(2,1)} all-to-all(bf16[64,14,2048]{2,1,0:T(8,128)(2,1)} %reshape.130), channel_id=1, replica_groups=mesh['expert'=64,'token'=4] {'expert'}, dimensions={0} | all-to-all | bytes 7340032 | tf_op jit(solution)/shard_map/all_to_all | solution.py:35
  422.7 6.0 reshape.131
  428.7 10.9 %convolution_convert_fusion = bf16[896,2048]{1,0:T(8,128)(2,1)} fusion(bf16[1,2048,768]{2,1,0:T(8,128)(2,1)S(1)} %copy-done, bf16[896,2048]{1,0:T(8,128)(2,1)} %reshape.131, bf16[1,2048,768]{2,1,0:T(8,128)(2,1)} %param.15, bf16[1,896,768]{2,1,0:T(8,128)(2,1)} %param.13), kind=kOutput, calls=%fused_computation.16 | convolution fusion | flops 5646548992 | bytes 15007744 | tf_op jit(solution)/shard_map/dot_general | solution.py:47
  439.6 6.0 reshape.132
  445.6 5.9 all-to-all-start.3
  451.6 0.1 reshape.136
  451.7 3.7 gather_fusion
  455.4 92.0 %all-to-all-done.3 = bf16[64,14,2048]{2,1,0:T(8,128)(2,1)} async-done(((bf16[64,14,2048]{2,1,0:T(8,128)(2,1)}), bf16[64,14,2048]{2,1,0:T(8,128)(2,1)}, u32[]{:S(2)}, u32[]{:S(2)}) %all-to-all-start.3) | async-done | bytes 3670048 | tf_op jit(solution)/shard_map/all_to_all | solution.py:51
  547.4 6.0 reshape.133
  553.4 8.8 %gather_fusion.4 = bf16[768,2048]{1,0:T(8,128)(2,1)S(1)} fusion(bf16[896,2048]{1,0:T(8,128)(2,1)} %reshape.133, s32[1024]{0:T(1024)S(1)} %pad_clamp_fusion.1), kind=kCustom, calls=%fused_computation.4.clone | custom fusion | bytes 6294528 | tf_op jit(solution)/shard_map/jit(_take)/gather | solution.py:54
  562.2 3.2 select_convert_fusion
  565.4 7.8 %reshape.142 = f32[128,6,2048]{2,1,0:T(8,128)} reshape(f32[768,2048]{1,0:T(8,128)} %select_convert_fusion) | data formatting | bytes 12582912 | tf_op jit(solution)/shard_map/reshape | solution.py:55
  573.3 0.0 copy-start.2
  573.3 6.7 multiply_reduce_fusion
  580.0 0.0 copy-done.2
  580.0 0.0 copy-done.3
  580.0 0.2 add_convert_fusion
  580.2 0.0 copy-start.4
  580.2 5.0 gather_fusion.5
  585.2 0.0 copy-done.4
  585.3 3.8 multiply_convert_fusion
  589.1 6.0 reshape.137
  595.1 6.1 all-to-all-start.4
  601.2 0.3 all-gather.2.cloned.1.call-start
  601.5 0.0 copy-done.5
  601.5 1.5 fusion.12
  603.0 0.0 all-gather.2.cloned.1.call-update
  603.1 94.0 %all-to-all-done.4 = bf16[64,14,2048]{2,1,0:T(8,128)(2,1)} async-done(((bf16[64,14,2048]{2,1,0:T(8,128)(2,1)}), bf16[64,14,2048]{2,1,0:T(8,128)(2,1)}, u32[]{:S(2)}, u32[]{:S(2)}) %all-to-all-start.4) | async-done | bytes 3670048 | tf_op jit(solution)/shard_map/all_to_all | solution.py:35
  697.0 8.9 %all_to_all.34 = bf16[896,4,512]{2,1,0:T(4,128)(2,1)} reshape(bf16[64,14,2048]{2,1,0:T(8,128)(2,1)} %all-to-all-done.4) | data formatting | bytes 7340032 | tf_op jit(solution)/shard_map/all_to_all | solution.py:80
  706.0 4.6 copy.26
  710.5 4.9 all-to-all-start.5
  715.5 41.3 %all-to-all-done.5 = bf16[896,4,512]{2,0,1:T(8,128)(2,1)} async-done(((bf16[896,4,512]{2,0,1:T(8,128)(2,1)}), bf16[896,4,512]{2,0,1:T(8,128)(2,1)}, u32[]{:S(2)}, u32[]{:S(2)}) %all-to-all-start.5) | async-done | bytes 3670048 | tf_op jit(solution)/shard_map/all_to_all | solution.py:80
  756.8 7.8 %fusion.18 = bf16[1,512,768]{2,1,0:T(8,128)(2,1)} fusion(bf16[3584,512]{1,0:T(8,128)(2,1)} %bitcast.6, bf16[3584,768]{1,0:T(8,128)(2,1)} %all-gather.2.cloned.1.call-done), kind=kOutput, calls=%fused_computation.39 | convolution fusion | flops 2819358720 | bytes 9961472 | tf_op jit(solution)/shard_map/dot_general | solution.py:81
  764.6 0.0 copy-done.1
  (14 shorter events, 0.1 us)
Async XLA Ops:
  7.2 138.5 %copy-start = (bf16[1,2048,768]{2,1,0:T(8,128)(2,1)S(1)}, bf16[1,2048,768]{2,1,0:T(8,128)(2,1)}, u32[]{:S(2)}) copy-start(bf16[1,2048,768]{2,1,0:T(8,128)(2,1)} %param.14) | copy-start | bytes 9437188
  162.6 6.5 copy-start.6
  162.6 102.2 %all-to-all-start.1 = ((bf16[64,14,2048]{2,1,0:T(8,128)(2,1)}), bf16[64,14,2048]{2,1,0:T(8,128)(2,1)}, u32[]{:S(2)}, u32[]{:S(2)}) async-start(bf16[64,14,2048]{2,1,0:T(8,128)(2,1)} %reshape.126), calls=%async_computation.1 | async-start | bytes 8388608 | tf_op jit(solution)/shard_map/all_to_all | solution.py:51
  445.6 101.8 %all-to-all-start.3 = ((bf16[64,14,2048]{2,1,0:T(8,128)(2,1)}), bf16[64,14,2048]{2,1,0:T(8,128)(2,1)}, u32[]{:S(2)}, u32[]{:S(2)}) async-start(bf16[64,14,2048]{2,1,0:T(8,128)(2,1)} %reshape.132), calls=%async_computation.3 | async-start | bytes 8388608 | tf_op jit(solution)/shard_map/all_to_all | solution.py:51
  573.3 6.7 copy-start.2
  573.3 6.7 copy-start.3
  580.2 5.0 copy-start.4
  595.1 6.4 copy-start.5
  595.1 101.9 %all-to-all-start.4 = ((bf16[64,14,2048]{2,1,0:T(8,128)(2,1)}), bf16[64,14,2048]{2,1,0:T(8,128)(2,1)}, u32[]{:S(2)}, u32[]{:S(2)}) async-start(bf16[64,14,2048]{2,1,0:T(8,128)(2,1)} %reshape.137), calls=%async_computation.4 | async-start | bytes 8388608 | tf_op jit(solution)/shard_map/all_to_all | solution.py:35
  601.2 114.3 %all-gather.2.cloned.1.call-start = ((), (), s32[]{:S(2)}) async-start(), calls=%async_computation.6 | async-start | bytes 6881280 | tf_op jit(solution)/shard_map/all_gather | solution.py:83
  710.5 46.3 %all-to-all-start.5 = ((bf16[896,4,512]{2,0,1:T(8,128)(2,1)}), bf16[896,4,512]{2,0,1:T(8,128)(2,1)}, u32[]{:S(2)}, u32[]{:S(2)}) async-start(bf16[896,4,512]{2,0,1:T(8,128)(2,1)} %copy.26), calls=%async_computation.5 | async-start | bytes 7340032 | tf_op jit(solution)/shard_map/all_to_all | solution.py:80
  756.8 7.8 %copy-start.1 = (bf16[1,2048,768]{2,1,0:T(8,128)(2,1)S(1)}, bf16[1,2048,768]{2,1,0:T(8,128)(2,1)}, u32[]{:S(2)}) copy-start(bf16[1,2048,768]{2,1,0:T(8,128)(2,1)} %param.14) | copy-start | bytes 9437188
Sparse Core Ops, SparseCore 0:
  603.8 60.5 all-gather.1
where the time goes:
time: 784 us; the launch traced here: 772 us
  waiting for transfers between devices  323 us (41%)
  blocking collectives  211 us (27%)
  local copies, waits for them, and re-layouts  132 us (17%)
  other arithmetic  38.3 us (5%)
  matrix products  29.7 us (4%)
  starting transfers between devices  23.7 us (3%)
  between operations  14.7 us (2%)
    all_to_all x2, blocking collectives, dispatch(): lax.all_to_all(shaped, 'expert', split_axis=0, concat_axis=0, tiled=True)  211 us
    all_to_all x2, waiting for transfers between devices, transpose_jacobian(): lax.all_to_all(shaped, 'expert', split_axis=0, concat_axis=0, tiled=True)  187 us
    all_to_all x1, waiting for transfers between devices, dispatch(): lax.all_to_all(shaped, 'expert', split_axis=0, concat_axis=0, tiled=True)  94 us
    all_to_all x1, waiting for transfers between devices, body(): lax.all_to_all(arrived, 'token', split_axis=1, concat_axis=0, tiled=True)  41.3 us
    dot_general x2, matrix products, transpose_jacobian(): lax.dot_general(scaled, up_weight, (((1,), (1,)), ((), ())), preferred_el...  21.9 us
    gather x2, local copies, waits for them, and re-layouts, transpose_jacobian(): picked = jnp.take(token_rows, route_of_slot // top_count, axis=0)  19.8 us
    gather x2, local copies, waits for them, and re-layouts, transpose_jacobian(): per_route = jnp.take(returned, target, axis=0).astype(jnp.float32)  18.5 us
    reshape x3, local copies, waits for them, and re-layouts, dispatch(): shaped = slot_rows.reshape(experts, -1, slot_rows.shape[1])  18 us
  transfers between devices with their start and end apart: 5, of which 4 were waited for; matrix products, arithmetic and copies ran while one was open for 1% of the time, Pallas kernels for 0%

commit v1 on v0

v1 whole, which is shorter than its diff:
```python
import jax
import jax.numpy as jnp
from jax import lax
from jax.experimental import pallas as pl
from jax.experimental.pallas import tpu as pltpu
from jax.sharding import PartitionSpec as P

grad_scale = 0.03125
root_half = 0.7071067811865476
inv_root_two_pi = 0.3989422804014327

NY, NZ, NC, NX = 4, 8, 2, 4
T = 128
D = 2048
HID = 768
CAP = 14
RB = NZ * CAP
NE = NY * NC
SL = NE * RB
H = 2
NCH = NX * H
W = D // NCH
ZR = NZ * T
NPF = 5
BF = jnp.bfloat16
F32 = jnp.float32
MESH = pl.DeviceIdType.MESH


def slope_and_act(hidden_rows):
    values = hidden_rows.astype(jnp.float32)
    normal_cdf = 0.5 * (1.0 + lax.erf(values * root_half))
    density = inv_root_two_pi * jnp.exp(-0.5 * values * values)
    slopes = normal_cdf + values * density
    active = (values * normal_cdf).astype(jnp.bfloat16)
    return (slopes, active)


def kernel(
    cot_hbm, tg_hbm, slope_hbm, act_hbm, up_hbm, down_hbm,
    ig_ref, dg_ref,
    CV, TV, TGR, SV, AX, UV, DV, PM, PT, G, ZB, YS, RL, RV, QL, QV, IA, SC, PF, RSS, RSR, XS, XR,
    l_zb, l_in, tg_s, tg_r, ax_s, ax_r,
    z_s, z_r, y_s, rl_r, f_s, rv_r, ql_r, qv_r, rs_s, rs_r, x_s, x_r,
):
    ex = lax.axis_index("expert")
    x = lax.axis_index("token")
    y = ex // (NZ * NC)
    z = (ex // NC) % NZ
    c = ex % NC
    me = y * NC + c
    yp, ym, y2 = (y + 1) % NY, (y + NY - 1) % NY, (y + 2) % NY

    def dev(yy, zz, cc, xx):
        return ((yy * NZ + zz) * NC + cc, xx)

    def remote(src, dst, ssem, rsem, target):
        return pltpu.make_async_remote_copy(
            src_ref=src, dst_ref=dst, send_sem=ssem, recv_sem=rsem, device_id=target, device_id_type=MESH
        )

    partner = dev(y, z, 1 - c, x)

    def wait_recv(ref, rsem):
        remote(ref, ref, tg_s.at[0], rsem, partner).wait_recv()

    def wait_send(ref, ssem):
        remote(ref, ref, ssem, tg_r.at[0], partner).wait_send()

    def col(i):
        return (i + x * H) % NCH

    def zrow(b):
        return pl.ds(pl.multiple_of(b * T, T), T)

    zme = zrow(z)

    def zb_in(i):
        return pltpu.make_async_copy(cot_hbm.at[col(i)], ZB.at[i, zme, :], l_zb.at[i])

    ins = [
        pltpu.make_async_copy(tg_hbm, TV, l_in.at[0]),
        pltpu.make_async_copy(down_hbm, DV, l_in.at[1]),
        pltpu.make_async_copy(slope_hbm, SV, l_in.at[2]),
        pltpu.make_async_copy(up_hbm, UV, l_in.at[3]),
        pltpu.make_async_copy(cot_hbm, CV, l_in.at[4]),
        pltpu.make_async_copy(act_hbm, AX.at[x], l_in.at[5]),
    ]
    ins[0].start()

    @pl.loop(0, NCH)
    def _(i):
        zb_in(i).start()

    for copy in ins[1:]:
        copy.start()
    ins[0].wait()

    @pl.loop(1, NX * NZ)
    def _(q):
        xx = (x + q // NZ) % NX
        zz = (z + q) % NZ
        remote(TV.at[zz], TGR.at[x, z], tg_s.at[0], tg_r.at[x], dev(y, zz, c, xx)).start()

    TGR[x, z] = TV[z]
    for dx in range(1, NX):
        remote(act_hbm, AX.at[x], ax_s.at[0], ax_r.at[x], dev(y, z, c, (x + dx) % NX)).start()

    @pl.loop(0, NCH)
    def _(i):
        for o in range(NE):
            QV[i, o * T + RB : (o + 1) * T, :] = jnp.zeros((T - RB, W), BF)

    def build(xs, with_pt):
        @pl.loop(0, NE)
        def _(o):
            gsum = jnp.zeros((RB, 1), F32)
            rows = pl.ds(pl.multiple_of(o * RB, 16), RB)
            for s in range(NZ):
                rank = TGR[xs, s, pl.ds(o, 1), :]
                gate = TGR[xs, s, pl.ds(NE + o, 1), :]
                slot = jnp.where(rank >= 0.0, rank + float(s * CAP), -1.0)
                iota = lax.broadcasted_iota(jnp.int32, (T, T), 0).astype(F32)
                hit = jnp.where(iota == slot, 1.0, 0.0)
                PM[rows, s * T : (s + 1) * T] = hit[:RB].astype(BF)
                gsum = gsum + jnp.sum(hit[:RB] * gate, axis=1, keepdims=True)
                if with_pt:
                    PT[s * T : (s + 1) * T, pl.ds(pl.multiple_of(o * T, T), T)] = hit.T.astype(BF)
            G[rows, :] = jnp.broadcast_to(gsum, (RB, 128))

    def y_send(i, dst, pitch, rsem, relay, relay_r):
        mine = dst.at[i, pl.ds(pl.multiple_of(me * pitch, 16), RB), :]

        def src(yy, cc):
            return YS.at[i, pl.ds(pl.multiple_of((yy * NC + cc) * RB, 16), RB), :]

        remote(src(y2, 0), relay.at[i, 0], y_s.at[i], relay_r.at[0, i], dev(yp, z, c, x)).start()
        remote(src(y2, 1), relay.at[i, 1], y_s.at[i], relay_r.at[1, i], dev(ym, z, c, x)).start()
        for cc in range(NC):
            remote(src(yp, cc), mine, y_s.at[i], rsem.at[me, i], dev(yp, z, cc, x)).start()
            remote(src(ym, cc), mine, y_s.at[i], rsem.at[me, i], dev(ym, z, cc, x)).start()
        remote(src(y, 1 - c), mine, y_s.at[i], rsem.at[me, i], partner).start()
        dst[i, pl.ds(pl.multiple_of(me * pitch, 16), RB), :] = YS[
            i, pl.ds(pl.multiple_of(me * RB, 16), RB), :
        ]

    def y_relay(i, dst, pitch, rsem, relay, relay_r):
        for d, (frm, to) in enumerate(((ym, yp), (yp, ym))):
            o = frm * NC + c
            wait_recv(relay.at[i, d], relay_r.at[d, i])
            remote(
                relay.at[i, d],
                dst.at[i, pl.ds(pl.multiple_of(o * pitch, 16), RB), :],
                f_s.at[i],
                rsem.at[o, i],
                dev(to, z, d, x),
            ).start()

    def y_wait(i, dst, pitch, rsem):
        for q in range(1, NE):
            o = (me + q) % NE
            wait_recv(dst.at[i, pl.ds(pl.multiple_of(o * pitch, 16), RB), :], rsem.at[o, i])

    def y_drain(relay):
        @pl.loop(0, NCH)
        def _(i):
            wait_send(YS.at[i, pl.ds(0, (NE - 1) * RB), :], y_s.at[i])
            wait_send(relay.at[i], f_s.at[i])

    SG = (1, -1)

    def lanes(k, d):
        return pl.ds(d * (W // 2), W // 2) if k == 4 else pl.ds(0, W)

    def z_send(i, k, d, src=None):
        b = (z + NZ - SG[d] * (k - 1)) % NZ
        ref = ZB.at[i, zrow(b), lanes(k, d)]
        remote(
            ref if src is None else src, ref, z_s.at[i], z_r.at[d, k - 1, i], dev(y, (z + NZ + SG[d]) % NZ, c, x)
        ).start()

    def z_wait(i, k, d):
        b = (z + NZ - SG[d] * k) % NZ
        wait_recv(ZB.at[i, zrow(b), lanes(k, d)], z_r.at[d, k - 1, i])

    def r_lanes(k, d):
        return pl.ds(d * (W // 2), W // 2) if k == 1 else pl.ds(0, W)

    def r_send(i, k, d):
        ln = r_lanes(k, d)
        remote(
            RSS.at[i, d, k - 1, :, ln],
            RSR.at[i, d, k - 1, :, ln],
            rs_s.at[i],
            rs_r.at[d, k - 1, i],
            dev(y, (z + NZ + SG[d]) % NZ, c, x),
        ).start()

    def r_wait(i, k, d):
        wait_recv(RSR.at[i, d, k - 1, :, r_lanes(k, d)], rs_r.at[d, k - 1, i])

    def when_chunk(t, lag):
        i = t - lag
        return i, pl.when((i >= 0) & (i < NCH))

    def dispatch(p, consume, last):
        @pl.loop(0, NCH + 6)
        def _(t):
            for k in (4, 3, 2):
                i, guard = when_chunk(t, k - 1)

                @guard
                def _(i=i, k=k):
                    for d in range(2):
                        z_wait(i, k - 1, d)
                        z_send(i, k, d)

            i, guard = when_chunk(t, 0)

            @guard
            def _(i=i):
                if last:
                    @pl.when(i >= H)
                    def _():
                        wait_recv(XR.at[i], x_r.at[i])

                    for d in range(2):
                        z_send(i, 1, d, XR.at[i])
                    ZB[i, zme, :] = XR[i]
                else:
                    @pl.when(p == 0)
                    def _():
                        zb_in(i).wait()

                    for d in range(2):
                        z_send(i, 1, d)

            if not last:
                @pl.when((p == 0) & (t == 2))
                def _():
                    wait_recv(TGR.at[x, pl.ds(0, NZ - 1)], tg_r.at[x])
                    for dx in range(1, NX):
                        xs = (x + dx) % NX
                        wait_recv(TGR.at[xs], tg_r.at[xs])
                    build(x, True)
                    for copy in ins[1:]:
                        copy.wait()

            i, guard = when_chunk(t, 5)

            @guard
            def _(i=i):
                y_relay(i, RV, RB, rv_r, RL, rl_r)

            i, guard = when_chunk(t, 4)

            @guard
            def _(i=i):
                for d in range(2):
                    z_wait(i, 4, d)
                if last:
                    @pl.when(i % H == 0)
                    def _():
                        build((x + NX - i // H) % NX, False)

                rows = jnp.dot(PM[...], ZB[i], preferred_element_type=F32)
                for n in range(W // 128):
                    YS[i, :, n * 128 : (n + 1) * 128] = (rows[:, n * 128 : (n + 1) * 128] * G[...]).astype(BF)
                y_send(i, RV, RB, rv_r, RL, rl_r)

            i, guard = when_chunk(t, 6)

            @guard
            def _(i=i):
                y_wait(i, RV, RB, rv_r)
                consume(i)

        @pl.loop(0, NCH)
        def _(i):
            wait_send(ZB.at[i, pl.ds(0, (NZ - 1) * T), :], z_s.at[i])

        y_drain(RL)

    def consume_inner(i):
        rows = pl.ds(pl.multiple_of(col(i) * W, W), W)

        @pl.loop(0, HID // 256)
        def _(n):
            ln = pl.ds(pl.multiple_of(n * 256, 256), 256)
            IA[:, ln] += jnp.dot(RV[i], DV[rows, ln], preferred_element_type=F32)

    def consume_grad(i):
        xs = (x + NX - i // H) % NX

        @pl.when((i % H == 0) & (i > 0))
        def _():
            wait_recv(AX.at[xs], ax_r.at[xs])

        rows = pl.ds(pl.multiple_of((i % H) * W, W), W)
        IA[rows, :] += lax.dot_general(RV[i], AX[xs], (((0,), (0,)), ((), ())), preferred_element_type=F32)

    def give_back(p):
        @pl.loop(0, NCH + 6)
        def _(t):
            i, guard = when_chunk(t, 6)

            @guard
            def _(i=i):
                for d in range(2):
                    r_wait(i, 4, d)
                total = PF[i % NPF, zme, :] + RSR[i, 0, 3].astype(F32) + RSR[i, 1, 3].astype(F32)
                term = total.astype(BF)

                @pl.when(p == 0)
                def _():
                    ZB[i, zme, :] = term

                @pl.when(p == 1)
                def _():
                    j = col(i)
                    grad = (CV[j].astype(F32) + ZB[i, zme, :].astype(F32) + term.astype(F32)).astype(BF)
                    ig_ref[:, pl.ds(pl.multiple_of(j * W, W), W)] = grad

                    @pl.when(i < H)
                    def _():
                        XR[i] = grad

                    @pl.when(i >= H)
                    def _():
                        XS[i] = grad
                        remote(
                            XS.at[i], XR.at[i], x_s.at[i], x_r.at[i], dev(y, z, c, (x + i // H) % NX)
                        ).start()

            for k in (4, 3, 2):
                i, guard = when_chunk(t, k + 1)

                @guard
                def _(i=i, k=k):
                    for d in range(2):
                        r_wait(i, k - 1, d)
                        mine = PF.at[i % NPF, zrow((z + NZ + SG[d] * (5 - k)) % NZ), :]
                        if k == 2:
                            half, rest = pl.ds(d * (W // 2), W // 2), pl.ds((1 - d) * (W // 2), W // 2)
                            RSS[i, d, 1, :, rest] = mine[:, rest].astype(BF)
                            RSS[i, d, 1, :, half] = (mine[:, half] + RSR[i, d, 0, :, half].astype(F32)).astype(BF)
                        else:
                            RSS[i, d, k - 1] = (mine[...] + RSR[i, d, k - 2].astype(F32)).astype(BF)
                        r_send(i, k, d)

            i, guard = when_chunk(t, 1)

            @guard
            def _(i=i):
                y_relay(i, QV, T, qv_r, QL, ql_r)

            i, guard = when_chunk(t, 2)

            @guard
            def _(i=i):
                y_wait(i, QV, T, qv_r)
                PF[i % NPF] = jnp.dot(PT[...], QV[i], preferred_element_type=F32)
                for d in range(2):
                    ln = pl.ds(d * (W // 2), W // 2)
                    RSS[i, d, 0, :, ln] = PF[i % NPF, zrow((z + 4) % NZ), ln].astype(BF)
                    r_send(i, 1, d)

            i, guard = when_chunk(t, 0)

            @guard
            def _(i=i):
                rows = pl.ds(pl.multiple_of(col(i) * W, W), W)
                YS[i] = lax.dot_general(
                    SC[...], UV[rows, :], (((1,), (1,)), ((), ())), preferred_element_type=F32
                ).astype(BF)
                y_send(i, QV, T, qv_r, QL, ql_r)

        @pl.loop(0, NCH)
        def _(i):
            wait_send(ZB.at[i, pl.ds(0, (NZ - 1) * T), :], rs_s.at[i])

        y_drain(QL)

    @pl.loop(0, 2)
    def _(p):
        IA[...] = jnp.zeros_like(IA)
        dispatch(p, consume_inner, False)

        @pl.loop(0, SL // 128)
        def _(n):
            rows = pl.ds(pl.multiple_of(n * 128, 128), 128)
            SC[rows, :] = (IA[rows, :] * SV[rows, :]).astype(BF)

        give_back(p)

    IA[: H * W, :] = jnp.zeros((H * W, HID), F32)
    dispatch(2, consume_grad, True)
    dg_ref[...] = (IA[: H * W, :] * grad_scale).astype(BF)

    @pl.loop(H, NCH)
    def _(i):
        wait_send(XS.at[i], x_s.at[i])

    for _ in range(NX - 1):
        wait_send(AX.at[x], ax_s.at[0])
    wait_send(TGR.at[pl.ds(0, NX - 1)], tg_s.at[0])
    wait_send(TGR.at[x, pl.ds(0, NZ - 1)], tg_s.at[0])


def body(cotangent, expert_ids, gate_values, hidden_pre, up_weight, down_weight):
    experts = NY * NZ * NC
    hidden = hidden_pre[0].reshape(NY, NZ, NC, CAP, HID).transpose(0, 2, 1, 3, 4).reshape(SL, HID)
    slopes, active = slope_and_act(hidden)
    onehot = expert_ids[:, :, None] == jnp.arange(experts, dtype=jnp.int32)[None, None, :]
    named = jnp.any(onehot, axis=1)
    count = named.astype(jnp.int32)
    rank = jnp.cumsum(count, axis=0) - count
    rank = jnp.where(named, rank, -1).astype(F32)
    gate = jnp.sum(jnp.where(onehot, gate_values[:, :, None], 0.0), axis=1)

    def planes(table):
        return table.T.reshape(NY, NZ, NC, T).transpose(1, 0, 2, 3).reshape(NZ, NE, T)

    tables = jnp.concatenate([planes(rank), planes(gate)], axis=1)
    cot = cotangent.reshape(T, NCH, W).transpose(1, 0, 2)

    vm, dma = pltpu.VMEM, pltpu.SemaphoreType.DMA
    input_grad, down_grad = pl.pallas_call(
        kernel,
        out_shape=(jax.ShapeDtypeStruct((T, D), BF), jax.ShapeDtypeStruct((H * W, HID), BF)),
        in_specs=[pl.BlockSpec(memory_space=pl.ANY)] * 6,
        out_specs=(pl.BlockSpec(memory_space=pltpu.VMEM),) * 2,
        scratch_shapes=[
            vm((NCH, T, W), BF),
            vm((NZ, 2 * NE, T), F32),
            vm((NX, NZ, 2 * NE, T), F32),
            vm((SL, HID), F32),
            vm((NX, SL, HID), BF),
            vm((D, HID), BF),
            vm((D, HID), BF),
            vm((SL, ZR), BF),
            vm((ZR, NE * T), BF),
            vm((SL, 128), F32),
            vm((NCH, ZR, W), BF),
            vm((NCH, SL, W), BF),
            vm((NCH, 2, RB, W), BF),
            vm((NCH, SL, W), BF),
            vm((NCH, 2, RB, W), BF),
            vm((NCH, NE * T, W), BF),
            vm((SL, HID), F32),
            vm((SL, HID), BF),
            vm((NPF, ZR, W), F32),
            vm((NCH, 2, 4, T, W), BF),
            vm((NCH, 2, 4, T, W), BF),
            vm((NCH, T, W), BF),
            vm((NCH, T, W), BF),
            dma((NCH,)), dma((6,)), dma((1,)), dma((NX,)), dma((1,)), dma((NX,)),
            dma((NCH,)), dma((2, 4, NCH)), dma((NCH,)), dma((2, NCH)), dma((NCH,)), dma((NE, NCH)),
            dma((2, NCH)), dma((NE, NCH)), dma((NCH,)), dma((2, 4, NCH)), dma((NCH,)), dma((NCH,)),
        ],
        compiler_params=pltpu.CompilerParams(has_side_effects=True, vmem_limit_bytes=67043328),
        name="layer",
    )(cot, tables, slopes, active, up_weight[0], down_weight[0])
    return (input_grad, down_grad[None])


def solution(mesh):
    in_specs = (
        P(("expert", "token"), None),
        P(("expert", "token"), None),
        P(("expert", "token"), None),
        P("expert", "token", None),
        P("expert", None, None),
        P("expert", None, None),
    )
    out_specs = (P(("expert", "token"), None), P("expert", "token", None))
    return jax.shard_map(body, mesh=mesh, in_specs=in_specs, out_specs=out_specs, check_vma=False)
```

time: 784 us -> 388 us (0.49); the launches traced: 772 us -> 388 us
  Pallas kernels: 0 us -> 368 us
  waiting for transfers between devices: 323 us -> 0 us
  blocking collectives: 211 us -> 0 us
  local copies, waits for them, and re-layouts: 132 us -> 12.7 us
  other arithmetic: 38.3 us -> 6.26 us
  matrix products: 29.7 us -> 0 us
  starting transfers between devices: 23.7 us -> 0 us
  between operations: 14.7 us -> 0.7 us
    pallas_call x0 -> x1, Pallas kernels: none -> 368 us  [body(): pl.pallas_call(kernel, out_shape=(jax.ShapeDtypeStruct((T, D), BF), jax.S...]
    all_to_all x4 -> x0, waiting for transfers between devices: 323 us -> none  [the longest x2 187 us: transpose_jacobian(): lax.all_to_all(shaped, 'expert', split_axis=0, concat_axis=0, tiled=True)]
    all_to_all x2 -> x0, blocking collectives: 211 us -> none  [dispatch(): lax.all_to_all(shaped, 'expert', split_axis=0, concat_axis=0, tiled=True)]
    reshape x13 -> x1, local copies, waits for them, and re-layouts: 69.9 us -> 1.01 us  [body(): cot = cotangent.reshape(T, NCH, W).transpose(1, 0, 2)]
    gather x6 -> x0, local copies, waits for them, and re-layouts: 46.9 us -> none  [the longest x2 19.8 us: transpose_jacobian(): picked = jnp.take(token_rows, route_of_slot // top_count, axis=0)]
    dot_general x3 -> x0, matrix products: 29.7 us -> none  [the longest x2 21.9 us: transpose_jacobian(): lax.dot_general(scaled, up_weight, (((1,), (1,)), ((), ())), preferred_el...]
    all_to_all x4 -> x0, starting transfers between devices: 23.5 us -> none  [the longest x2 12.5 us: transpose_jacobian(): lax.all_to_all(shaped, 'expert', split_axis=0, concat_axis=0, tiled=True)]
    reduce_sum x4 -> x1, other arithmetic: 14.6 us -> 0.73 us  [body(): gate = jnp.sum(jnp.where(onehot, gate_values[:, :, None], 0.0), axis=1)]
  transfers between devices with their start and end apart: 5 -> 0, of which waited for: 4 -> 0; matrix products, arithmetic and copies ran while one was open for 1% -> 0% of each run, Pallas kernels for 0% -> 0%
where the time goes in v1:
time: 388 us
  Pallas kernels  368 us (95%)
  local copies, waits for them, and re-layouts  12.7 us (3%)
  other arithmetic  6.26 us (2%)
    pallas_call x1, Pallas kernels, body(): pl.pallas_call(kernel, out_shape=(jax.ShapeDtypeStruct((T, D), BF), jax.S...  368 us

profile of v1, /device:TPU:7, one launch (start us, length us, event | category | flops | bytes accessed | tf_op | source)
XLA Modules:
  0.0 387.8 jit_solution(17208897198051381485)
XLA Ops:
  0.6 0.7 fusion.4
  1.4 0.1 copy.30
  1.5 0.2 reduce_window_sum.13
  1.6 0.1 copy.31
  1.8 0.7 select_reduce_fusion
  2.5 0.6 pad_maximum_fusion.tg_hbm
  3.1 3.4 reshape.32
  6.5 2.1 copy.34
  8.7 1.7 reshape.31
  10.4 0.0 copy-start
  10.4 4.0 %multiply_convert_fusion = (bf16[896,768]{1,0:T(8,128)(2,1)}, f32[896,768]{1,0:T(8,128)}) fusion(f32[896,768]{1,0:T(8,128)} %reshape.31), kind=kLoop, calls=%fused_computation.5 | loop fusion | flops 6881280 | bytes 6881280 | tf_op jit(solution)/shard_map/convert_element_type | solution.py:35
  14.4 0.0 copy-done
  14.4 0.3 copy.28
  14.7 1.0 copy.29
  15.7 368.2 %layer.1 = (bf16[128,2048]{1,0:T(8,128)(2,1)}, bf16[512,768]{1,0:T(8,128)(2,1)}) custom-call(bf16[8,128,256]{2,1,0:T(8,128)(2,1)} %bitcast.28, f32[8,16,128]{2,1,0:T(8,128)} %pad_maximum_fusion.tg_hbm, f32[896,768]{1,0:T(8,128)} %get-tuple-element.7.slope_hbm, bf16[896,768]{1,0:T(8,128)(2,1)} %get-tuple-element.6.act_hbm, bf16[2048,768]{1,0:T(8,128)(2,1)} %bitcast.25, ...), custom_call_target="tpu_custom_call" | custom-call | tf_op jit(solution)/shard_map/layer/pallas_call | solution.py:428
  383.9 1.9 copy.37
  385.8 2.1 copy.38
  (4 shorter events, 0.1 us)
Async XLA Ops:
  10.4 4.0 %copy-start = (bf16[128,2048]{1,0:T(8,128)(2,1)S(1)}, bf16[128,2048]{1,0:T(8,128)(2,1)}, u32[]{:S(2)}) copy-start(bf16[128,2048]{1,0:T(8,128)(2,1)} %param.6) | copy-start | bytes 1572868

commit v2 on v1

v2 whole, which is shorter than its diff:
```python
import jax
import jax.numpy as jnp
from jax import lax
from jax.experimental import pallas as pl
from jax.experimental.pallas import tpu as pltpu
from jax.sharding import PartitionSpec as P

grad_scale = 0.03125
root_half = 0.7071067811865476
inv_root_two_pi = 0.3989422804014327

NY, NZ, NC, NX = 4, 8, 2, 4
T = 128
D = 2048
HID = 768
CAP = 14
RB = NZ * CAP
NE = NY * NC
SL = NE * RB
H = 2
NCH = NX * H
W = D // NCH
ZR = NZ * T
NPF = 5
BF = jnp.bfloat16
F32 = jnp.float32
MESH = pl.DeviceIdType.MESH


def slope_and_act(hidden_rows):
    values = hidden_rows
    normal_cdf = 0.5 * (1.0 + lax.erf(values * root_half))
    density = inv_root_two_pi * jnp.exp(-0.5 * values * values)
    slopes = normal_cdf + values * density
    active = (values * normal_cdf).astype(jnp.bfloat16)
    return (slopes, active)


def kernel(
    cot_hbm, tg_hbm, hid_hbm, up_hbm, down_hbm,
    ig_ref, dg_ref,
    CV, TV, TGR, HV, SV, AX, UV, DV, PM, PT, G, ZB, YS, RL, RV, QL, QV, IA, SC, PF, RSS, RSR, XS, XR,
    l_zb, l_in, tg_s, tg_r, ax_s, ax_r,
    z_s, z_r, y_s, rl_r, f_s, g_s, rv_r, ql_r, qv_r, rs_s, rs_r, x_s, x_r,
):
    ex = lax.axis_index("expert")
    x = lax.axis_index("token")
    y = ex // (NZ * NC)
    z = (ex // NC) % NZ
    c = ex % NC
    me = y * NC + c
    yp, ym, y2 = (y + 1) % NY, (y + NY - 1) % NY, (y + 2) % NY

    def dev(yy, zz, cc, xx):
        return ((yy * NZ + zz) * NC + cc, xx)

    def remote(src, dst, ssem, rsem, target):
        return pltpu.make_async_remote_copy(
            src_ref=src, dst_ref=dst, send_sem=ssem, recv_sem=rsem, device_id=target, device_id_type=MESH
        )

    partner = dev(y, z, 1 - c, x)

    def wait_recv(ref, rsem):
        remote(ref, ref, tg_s.at[0], rsem, partner).wait_recv()

    def wait_send(ref, ssem):
        remote(ref, ref, ssem, tg_r.at[0], partner).wait_send()

    def col(i):
        return (i + x * H) % NCH

    def wide(j):
        return pl.ds(pl.multiple_of(j * W, W), W)

    def zrow(b):
        return pl.ds(pl.multiple_of(b * T, T), T)

    zme = zrow(z)

    def zb_in(i):
        return pltpu.make_async_copy(cot_hbm.at[:, wide(col(i))], ZB.at[i, zme, :], l_zb.at[i])

    ins = [
        pltpu.make_async_copy(tg_hbm, TV, l_in.at[0]),
        pltpu.make_async_copy(hid_hbm, HV, l_in.at[1]),
        pltpu.make_async_copy(down_hbm, DV, l_in.at[2]),
        pltpu.make_async_copy(up_hbm, UV, l_in.at[3]),
        pltpu.make_async_copy(cot_hbm, CV, l_in.at[4]),
    ]
    ins[0].start()

    @pl.loop(0, NCH)
    def _(i):
        zb_in(i).start()

    for copy in ins[1:]:
        copy.start()
    ins[0].wait()

    @pl.loop(1, NX * NZ)
    def _(q):
        xx = (x + q // NZ) % NX
        zz = (z + q) % NZ
        remote(TV.at[zz], TGR.at[x, z], tg_s.at[0], tg_r.at[x], dev(y, zz, c, xx)).start()

    TGR[x, z] = TV[z]
    @pl.loop(0, NCH)
    def _(i):
        for o in range(NE):
            QV[i, o * T + RB : (o + 1) * T, :] = jnp.zeros((T - RB, W), BF)

    YB = NZ * NC * CAP

    def activate(b):
        new = lax.broadcasted_iota(jnp.int32, (YB, YB), 0).astype(F32)
        core = jnp.where(new >= float(RB), 1.0, 0.0)
        new = new - core * RB
        plane = jnp.floor((new + 0.5) * (1.0 / CAP))
        old = plane * (NC * CAP) + core * CAP + (new - plane * CAP)
        here = lax.broadcasted_iota(jnp.int32, (YB, YB), 1).astype(F32)
        order = jnp.where(here == old, 1.0, 0.0).astype(BF)
        rows = pl.ds(b * YB, YB)
        hidden = jnp.dot(order, HV[rows, :], preferred_element_type=F32)
        slopes, active = slope_and_act(hidden)
        SV[rows, :] = slopes
        AX[x, rows, :] = active

    def build(xs, with_pt):
        @pl.loop(0, NE)
        def _(o):
            gsum = jnp.zeros((RB, 1), F32)
            rows = pl.ds(pl.multiple_of(o * RB, 16), RB)
            for s in range(NZ):
                rank = TGR[xs, s, pl.ds(o, 1), :]
                gate = TGR[xs, s, pl.ds(NE + o, 1), :]
                slot = jnp.where(rank >= 0.0, rank + float(s * CAP), -1.0)
                iota = lax.broadcasted_iota(jnp.int32, (T, T), 0).astype(F32)
                hit = jnp.where(iota == slot, 1.0, 0.0)
                PM[rows, s * T : (s + 1) * T] = hit[:RB].astype(BF)
                gsum = gsum + jnp.sum(hit[:RB] * gate, axis=1, keepdims=True)
                if with_pt:
                    PT[s * T : (s + 1) * T, pl.ds(pl.multiple_of(o * T, T), T)] = hit.T.astype(BF)
            G[rows, :] = jnp.broadcast_to(gsum, (RB, 128))

    def y_send(i, dst, pitch, rsem, relay, relay_r):
        mine = dst.at[i, pl.ds(pl.multiple_of(me * pitch, 16), RB), :]

        def src(yy, cc):
            return YS.at[i, pl.ds(pl.multiple_of((yy * NC + cc) * RB, 16), RB), :]

        remote(src(y2, 0), relay.at[i, 0], y_s.at[i], relay_r.at[0, i], dev(yp, z, c, x)).start()
        remote(src(y2, 1), relay.at[i, 1], y_s.at[i], relay_r.at[1, i], dev(ym, z, c, x)).start()
        for cc in range(NC):
            remote(src(yp, cc), mine, y_s.at[i], rsem.at[me, i], dev(yp, z, cc, x)).start()
            remote(src(ym, cc), mine, y_s.at[i], rsem.at[me, i], dev(ym, z, cc, x)).start()
        remote(src(y, 1 - c), mine, y_s.at[i], rsem.at[me, i], partner).start()
        dst[i, pl.ds(pl.multiple_of(me * pitch, 16), RB), :] = YS[
            i, pl.ds(pl.multiple_of(me * RB, 16), RB), :
        ]

    def y_relay(i, dst, pitch, rsem, relay, relay_r, fsem):
        for d, (frm, to) in enumerate(((ym, yp), (yp, ym))):
            o = frm * NC + c
            wait_recv(relay.at[i, d], relay_r.at[d, i])
            remote(
                relay.at[i, d],
                dst.at[i, pl.ds(pl.multiple_of(o * pitch, 16), RB), :],
                fsem.at[i],
                rsem.at[o, i],
                dev(to, z, d, x),
            ).start()

    def y_wait(i, dst, pitch, rsem):
        for q in range(1, NE):
            o = (me + q) % NE
            wait_recv(dst.at[i, pl.ds(pl.multiple_of(o * pitch, 16), RB), :], rsem.at[o, i])

    SG = (1, -1)

    def lanes(k, d):
        return pl.ds(d * (W // 2), W // 2) if k == 4 else pl.ds(0, W)

    def z_send(i, k, d, src=None):
        b = (z + NZ - SG[d] * (k - 1)) % NZ
        ref = ZB.at[i, zrow(b), lanes(k, d)]
        remote(
            ref if src is None else src, ref, z_s.at[i], z_r.at[d, k - 1, i], dev(y, (z + NZ + SG[d]) % NZ, c, x)
        ).start()

    def z_wait(i, k, d):
        b = (z + NZ - SG[d] * k) % NZ
        wait_recv(ZB.at[i, zrow(b), lanes(k, d)], z_r.at[d, k - 1, i])

    def r_lanes(k, d):
        return pl.ds(d * (W // 2), W // 2) if k == 1 else pl.ds(0, W)

    def r_send(i, k, d):
        ln = r_lanes(k, d)
        remote(
            RSS.at[i, d, k - 1, :, ln],
            RSR.at[i, d, k - 1, :, ln],
            rs_s.at[i],
            rs_r.at[d, k - 1, i],
            dev(y, (z + NZ + SG[d]) % NZ, c, x),
        ).start()

    def r_wait(i, k, d):
        wait_recv(RSR.at[i, d, k - 1, :, r_lanes(k, d)], rs_r.at[d, k - 1, i])

    def at_chunk(t, lag):
        i = t - lag

        def run(f):
            @pl.when((i >= 0) & (i < NCH))
            def _():
                f(i)

        return run

    def d_rings(p, t, lag):
        for k in (4, 3, 2):
            @at_chunk(t, lag + k - 1)
            def _(i, k=k):
                for d in range(2):
                    z_wait(i, k - 1, d)
                    z_send(i, k, d)

        @at_chunk(t, lag)
        def _(i):
            if p == 0:
                zb_in(i).wait()
            if p == 2:
                @pl.when(i >= H)
                def _():
                    wait_recv(XR.at[i], x_r.at[i])

            for d in range(2):
                z_send(i, 1, d, XR.at[i] if p == 2 else None)
            if p == 2:
                ZB[i, zme, :] = XR[i]

    def d_relay(p, t, lag):
        @at_chunk(t, lag + 5)
        def _(i):
            y_relay(i, RV, RB, rv_r, RL, rl_r, f_s)

    def d_select(p, t, lag):
        @at_chunk(t, lag + 4)
        def _(i):
            for d in range(2):
                z_wait(i, 4, d)
            if p == 2:
                @pl.when(i % H == 0)
                def _():
                    build((x + NX - i // H) % NX, False)
            if p > 0:
                y_sent(i)

            rows = jnp.dot(PM[...], ZB[i], preferred_element_type=F32)
            for n in range(W // 128):
                YS[i, :, n * 128 : (n + 1) * 128] = (rows[:, n * 128 : (n + 1) * 128] * G[...]).astype(BF)
            y_send(i, RV, RB, rv_r, RL, rl_r)

    def d_consume(p, t, lag):
        @at_chunk(t, lag + 6)
        def _(i):
            y_wait(i, RV, RB, rv_r)
            (consume_grad if p == 2 else consume_inner)(i)

    def y_sent(i):
        wait_send(YS.at[i, pl.ds(0, (NE - 1) * RB), :], y_s.at[i])

    def d_sent():
        @pl.loop(0, NCH)
        def _(i):
            wait_send(ZB.at[i, pl.ds(0, (NZ - 1) * T), :], z_s.at[i])
            wait_send(RL.at[i], f_s.at[i])
            y_sent(i)

    def consume_inner(i):
        rows = wide(col(i))

        @pl.loop(0, HID // 256)
        def _(n):
            ln = pl.ds(pl.multiple_of(n * 256, 256), 256)
            IA[:, ln] += jnp.dot(RV[i], DV[rows, ln], preferred_element_type=F32)

    def consume_grad(i):
        xs = (x + NX - i // H) % NX

        @pl.when((i % H == 0) & (i > 0))
        def _():
            wait_recv(AX.at[xs], ax_r.at[xs])

        rows = pl.ds(pl.multiple_of((i % H) * W, W), W)
        IA[rows, :] += lax.dot_general(RV[i], AX[xs], (((0,), (0,)), ((), ())), preferred_element_type=F32)

    def r_final(p, t):
        @at_chunk(t, 6)
        def _(i):
            for d in range(2):
                r_wait(i, 4, d)
            total = PF[i % NPF, zme, :] + RSR[i, 0, 3].astype(F32) + RSR[i, 1, 3].astype(F32)
            term = total.astype(BF)
            if p == 1:
                ZB[i, zme, :] = term
            else:
                lanes_j = wide(col(i))
                grad = (
                    CV[:, lanes_j].astype(F32) + ZB[i, zme, :].astype(F32) + term.astype(F32)
                ).astype(BF)
                ig_ref[:, lanes_j] = grad

                @pl.when(i < H)
                def _():
                    XR[i] = grad

                @pl.when(i >= H)
                def _():
                    XS[i] = grad
                    remote(
                        XS.at[i], XR.at[i], x_s.at[i], x_r.at[i], dev(y, z, c, (x + i // H) % NX)
                    ).start()

    def r_rings(t):
        for k in (4, 3, 2):
            @at_chunk(t, k + 1)
            def _(i, k=k):
                for d in range(2):
                    r_wait(i, k - 1, d)
                    mine = PF.at[i % NPF, zrow((z + NZ + SG[d] * (5 - k)) % NZ), :]
                    if k == 2:
                        half, rest = pl.ds(d * (W // 2), W // 2), pl.ds((1 - d) * (W // 2), W // 2)
                        RSS[i, d, 1, :, rest] = mine[:, rest].astype(BF)
                        RSS[i, d, 1, :, half] = (mine[:, half] + RSR[i, d, 0, :, half].astype(F32)).astype(BF)
                    else:
                        RSS[i, d, k - 1] = (mine[...] + RSR[i, d, k - 2].astype(F32)).astype(BF)
                    r_send(i, k, d)

    def r_relay(t):
        @at_chunk(t, 1)
        def _(i):
            y_relay(i, QV, T, qv_r, QL, ql_r, g_s)

        @at_chunk(t, 3)
        def _(i):
            wait_send(QL.at[i], g_s.at[i])

    def r_combine(t):
        @at_chunk(t, 2)
        def _(i):
            y_wait(i, QV, T, qv_r)
            PF[i % NPF] = jnp.dot(PT[...], QV[i], preferred_element_type=F32)
            for d in range(2):
                ln = pl.ds(d * (W // 2), W // 2)
                RSS[i, d, 0, :, ln] = PF[i % NPF, zrow((z + 4) % NZ), ln].astype(BF)
                r_send(i, 1, d)

    def r_piece(t):
        @at_chunk(t, 0)
        def _(i):
            YS[i] = lax.dot_general(
                SC[...], UV[wide(col(i)), :], (((1,), (1,)), ((), ())), preferred_element_type=F32
            ).astype(BF)
            y_send(i, QV, T, qv_r, QL, ql_r)

    def r_sent():
        @pl.loop(0, NCH)
        def _(i):
            wait_send(ZB.at[i, pl.ds(0, (NZ - 1) * T), :], rs_s.at[i])

    def scale_inner():
        @pl.loop(0, SL // 128)
        def _(n):
            rows = pl.ds(pl.multiple_of(n * 128, 128), 128)
            SC[rows, :] = (IA[rows, :] * SV[rows, :]).astype(BF)
            IA[rows, :] = jnp.zeros((128, HID), F32)

    IA[...] = jnp.zeros_like(IA)

    @pl.loop(0, NCH + 6)
    def _(t):
        d_rings(0, t, 0)

        @pl.when(t == 2)
        def _():
            wait_recv(TGR.at[x, pl.ds(0, NZ - 1)], tg_r.at[x])
            for dx in range(1, NX):
                xs = (x + dx) % NX
                wait_recv(TGR.at[xs], tg_r.at[xs])
            build(x, True)

        @pl.when(t == 0)
        def _():
            ins[1].wait()

        @pl.when(t < NY)
        def _():
            activate(t)

        @pl.when(t == NY)
        def _():
            for copy in ins[2:]:
                copy.wait()
            for dx in range(1, NX):
                remote(AX.at[x], AX.at[x], ax_s.at[0], ax_r.at[x], dev(y, z, c, (x + dx) % NX)).start()

        d_relay(0, t, 0)
        d_select(0, t, 0)
        d_consume(0, t, 0)

    d_sent()

    for p in (1, 2):
        lag = 5 + p
        scale_inner()

        @pl.loop(0, NCH + 6 + lag)
        def _(t, p=p, lag=lag):
            r_final(p, t)
            r_rings(t)
            d_rings(p, t, lag)
            r_relay(t)
            d_relay(p, t, lag)
            r_combine(t)
            d_select(p, t, lag)
            r_piece(t)
            d_consume(p, t, lag)

        r_sent()
        d_sent()

    dg_ref[...] = (IA[: H * W, :] * grad_scale).astype(BF)

    @pl.loop(H, NCH)
    def _(i):
        wait_send(XS.at[i], x_s.at[i])

    for _ in range(NX - 1):
        wait_send(AX.at[x], ax_s.at[0])
    wait_send(TGR.at[pl.ds(0, NX - 1)], tg_s.at[0])
    wait_send(TGR.at[x, pl.ds(0, NZ - 1)], tg_s.at[0])


def body(cotangent, expert_ids, gate_values, hidden_pre, up_weight, down_weight):
    experts = NY * NZ * NC
    onehot = expert_ids[:, :, None] == jnp.arange(experts, dtype=jnp.int32)[None, None, :]
    named = jnp.any(onehot, axis=1)
    count = named.astype(jnp.int32)
    rank = jnp.cumsum(count, axis=0) - count
    rank = jnp.where(named, rank, -1).astype(F32)
    gate = jnp.sum(jnp.where(onehot, gate_values[:, :, None], 0.0), axis=1)

    def planes(table):
        return table.T.reshape(NY, NZ, NC, T).transpose(1, 0, 2, 3).reshape(NZ, NE, T)

    tables = jnp.concatenate([planes(rank), planes(gate)], axis=1)
    vm, dma = pltpu.VMEM, pltpu.SemaphoreType.DMA
    input_grad, down_grad = pl.pallas_call(
        kernel,
        out_shape=(jax.ShapeDtypeStruct((T, D), BF), jax.ShapeDtypeStruct((H * W, HID), BF)),
        in_specs=[pl.BlockSpec(memory_space=pl.ANY)] * 5,
        out_specs=(pl.BlockSpec(memory_space=pltpu.VMEM),) * 2,
        scratch_shapes=[
            vm((T, D), BF),
            vm((NZ, 2 * NE, T), F32),
            vm((NX, NZ, 2 * NE, T), F32),
            vm((SL, HID), BF),
            vm((SL, HID), F32),
            vm((NX, SL, HID), BF),
            vm((D, HID), BF),
            vm((D, HID), BF),
            vm((SL, ZR), BF),
            vm((ZR, NE * T), BF),
            vm((SL, 128), F32),
            vm((NCH, ZR, W), BF),
            vm((NCH, SL, W), BF),
            vm((NCH, 2, RB, W), BF),
            vm((NCH, SL, W), BF),
            vm((NCH, 2, RB, W), BF),
            vm((NCH, NE * T, W), BF),
            vm((SL, HID), F32),
            vm((SL, HID), BF),
            vm((NPF, ZR, W), F32),
            vm((NCH, 2, 4, T, W), BF),
            vm((NCH, 2, 4, T, W), BF),
            vm((NCH, T, W), BF),
            vm((NCH, T, W), BF),
            dma((NCH,)), dma((5,)), dma((1,)), dma((NX,)), dma((1,)), dma((NX,)),
            dma((NCH,)), dma((2, 4, NCH)), dma((NCH,)), dma((2, NCH)), dma((NCH,)), dma((NCH,)), dma((NE, NCH)),
            dma((2, NCH)), dma((NE, NCH)), dma((NCH,)), dma((2, 4, NCH)), dma((NCH,)), dma((NCH,)),
        ],
        compiler_params=pltpu.CompilerParams(has_side_effects=True, vmem_limit_bytes=67043328),
        name="layer",
    )(cotangent, tables, hidden_pre[0], up_weight[0], down_weight[0])
    return (input_grad, down_grad[None])


def solution(mesh):
    in_specs = (
        P(("expert", "token"), None),
        P(("expert", "token"), None),
        P(("expert", "token"), None),
        P("expert", "token", None),
        P("expert", None, None),
        P("expert", None, None),
    )
    out_specs = (P(("expert", "token"), None), P("expert", "token", None))
    return jax.shard_map(body, mesh=mesh, in_specs=in_specs, out_specs=out_specs, check_vma=False)
```

time: 388 us -> 341 us (0.88)
  Pallas kernels: 368 us -> 333 us
  local copies, waits for them, and re-layouts: 12.7 us -> 4.12 us
  other arithmetic: 6.26 us -> 2.3 us
    pallas_call x1, Pallas kernels: 368 us -> 333 us  [body(): pl.pallas_call(kernel, out_shape=(jax.ShapeDtypeStruct((T, D), BF), jax.S...]
    convert_element_type x3 -> x0, local copies, waits for them, and re-layouts: 7.29 us -> none  [slope_and_act(): values = hidden_rows.astype(jnp.float32)]
    convert_element_type x1 -> x0, other arithmetic: 3.97 us -> none  [slope_and_act(): active = (values * normal_cdf).astype(jnp.bfloat16)]
where the time goes in v2:
time: 341 us; the launch traced here: 340 us
  Pallas kernels  333 us (98%)
  local copies, waits for them, and re-layouts  4.12 us (1%)
    pallas_call x1, Pallas kernels, body(): pl.pallas_call(kernel, out_shape=(jax.ShapeDtypeStruct((T, D), BF), jax.S...  333 us

profile of v2, /device:TPU:7, one launch (start us, length us, event | category | flops | bytes accessed | tf_op | source)
XLA Modules:
  0.0 340.0 jit_solution(10611732942167553040)
XLA Ops:
  0.6 0.7 fusion
  1.4 0.1 copy.21
  1.5 0.2 reduce_window_sum.13
  1.6 0.1 copy.22
  1.8 0.7 select_reduce_fusion
  2.5 0.6 pad_maximum_fusion.tg_hbm
  3.1 332.9 %layer.1 = (bf16[128,2048]{1,0:T(8,128)(2,1)}, bf16[512,768]{1,0:T(8,128)(2,1)}) custom-call(bf16[128,2048]{1,0:T(8,128)(2,1)} %cot_hbm.1, f32[8,16,128]{2,1,0:T(8,128)} %pad_maximum_fusion.tg_hbm, bf16[896,768]{1,0:T(8,128)(2,1)} %bitcast.24, bf16[2048,768]{1,0:T(8,128)(2,1)} %bitcast.22, bf16[2048,768]{1,0:T(8,128)(2,1)} %bitcast.23), custom_call_target="tpu_custom_call" | custom-call | tf_op jit(solution)/shard_map/layer/pallas_call | solution.py:460
  336.0 1.9 copy.27
  337.9 2.1 copy.28
  (4 shorter events, 0.1 us)

commit v3 on v2

--- a/solution.py
+++ b/solution.py
@@ -37,9 +37,9 @@
 
 
 def kernel(
-    cot_hbm, tg_hbm, hid_hbm, up_hbm, down_hbm,
+    cot_hbm, id_hbm, gate_hbm, hid_hbm, up_hbm, down_hbm,
     ig_ref, dg_ref,
-    CV, TV, TGR, HV, SV, AX, UV, DV, PM, PT, G, ZB, YS, RL, RV, QL, QV, IA, SC, PF, RSS, RSR, XS, XR,
+    CV, IDV, GTV, TV, TGR, HV, SV, AX, UV, DV, PM, PT, G, ZB, YS, RL, RV, QL, QV, IA, SC, PF, RSS, RSR, XS, XR,
     l_zb, l_in, tg_s, tg_r, ax_s, ax_r,
     z_s, z_r, y_s, rl_r, f_s, g_s, rv_r, ql_r, qv_r, rs_s, rs_r, x_s, x_r,
 ):
@@ -78,37 +78,64 @@
 
     zme = zrow(z)
 
+    barrier = pltpu.get_barrier_semaphore()
+
+    def greet(target):
+        pl.semaphore_signal(barrier, inc=1, device_id=target, device_id_type=MESH)
+
+    @pl.loop(1, NX * NZ)
+    def _(q):
+        greet(dev(y, (z + q) % NZ, c, (x + q // NZ) % NX))
+
+    for cc in range(NC):
+        greet(dev(yp, z, cc, x))
+        greet(dev(ym, z, cc, x))
+    greet(partner)
+
     def zb_in(i):
         return pltpu.make_async_copy(cot_hbm.at[:, wide(col(i))], ZB.at[i, zme, :], l_zb.at[i])
 
     ins = [
-        pltpu.make_async_copy(tg_hbm, TV, l_in.at[0]),
-        pltpu.make_async_copy(hid_hbm, HV, l_in.at[1]),
-        pltpu.make_async_copy(down_hbm, DV, l_in.at[2]),
-        pltpu.make_async_copy(up_hbm, UV, l_in.at[3]),
-        pltpu.make_async_copy(cot_hbm, CV, l_in.at[4]),
+        pltpu.make_async_copy(id_hbm, IDV, l_in.at[0]),
+        pltpu.make_async_copy(gate_hbm, GTV, l_in.at[1]),
+        pltpu.make_async_copy(hid_hbm, HV, l_in.at[2]),
+        pltpu.make_async_copy(down_hbm, DV, l_in.at[3]),
+        pltpu.make_async_copy(up_hbm, UV, l_in.at[4]),
+        pltpu.make_async_copy(cot_hbm, CV, l_in.at[5]),
     ]
-    ins[0].start()
+    for copy in ins[:3]:
+        copy.start()
 
     @pl.loop(0, NCH)
     def _(i):
         zb_in(i).start()
 
-    for copy in ins[1:]:
+    for copy in ins[3:]:
         copy.start()
-    ins[0].wait()
-
-    @pl.loop(1, NX * NZ)
-    def _(q):
-        xx = (x + q // NZ) % NX
-        zz = (z + q) % NZ
-        remote(TV.at[zz], TGR.at[x, z], tg_s.at[0], tg_r.at[x], dev(y, zz, c, xx)).start()
-
-    TGR[x, z] = TV[z]
+
     @pl.loop(0, NCH)
     def _(i):
         for o in range(NE):
             QV[i, o * T + RB : (o + 1) * T, :] = jnp.zeros((T - RB, W), BF)
+
+    IA[...] = jnp.zeros_like(IA)
+
+    def tabulate():
+        row = lax.broadcasted_iota(jnp.int32, (NZ * NE, T), 0)
+        expert = (((row >> 1) & (NY - 1)) * NZ + (row >> 3)) * NC + (row & (NC - 1))
+        named, gate = jnp.zeros((NZ * NE, T), F32), jnp.zeros((NZ * NE, T), F32)
+        for k in range(IDV.shape[0]):
+            hit = IDV[k : k + 1, :] == expert
+            named = jnp.where(hit, 1.0, named)
+            gate = jnp.where(hit, GTV[k : k + 1, :], gate)
+        first = lax.broadcasted_iota(jnp.int32, (T, T), 0)
+        second = lax.broadcasted_iota(jnp.int32, (T, T), 1)
+        before = jnp.where(first < second, 1.0, 0.0).astype(BF)
+        rank = jnp.dot(named.astype(BF), before, preferred_element_type=F32)
+        rank = jnp.where(named > 0.0, rank, -1.0)
+        for zz in range(NZ):
+            TV[zz, :NE, :] = rank[zz * NE : (zz + 1) * NE]
+            TV[zz, NE:, :] = gate[zz * NE : (zz + 1) * NE]
 
     YB = NZ * NC * CAP
 
@@ -218,16 +245,14 @@
 
         return run
 
-    def d_rings(p, t, lag):
-        for k in (4, 3, 2):
-            @at_chunk(t, lag + k - 1)
-            def _(i, k=k):
+    def d_ring(p, t, lag, k):
+        @at_chunk(t, lag)
+        def _(i):
+            if k > 1:
                 for d in range(2):
                     z_wait(i, k - 1, d)
                     z_send(i, k, d)
-
-        @at_chunk(t, lag)
-        def _(i):
+                return
             if p == 0:
                 zb_in(i).wait()
             if p == 2:
@@ -241,12 +266,12 @@
                 ZB[i, zme, :] = XR[i]
 
     def d_relay(p, t, lag):
-        @at_chunk(t, lag + 5)
+        @at_chunk(t, lag)
         def _(i):
             y_relay(i, RV, RB, rv_r, RL, rl_r, f_s)
 
     def d_select(p, t, lag):
-        @at_chunk(t, lag + 4)
+        @at_chunk(t, lag)
         def _(i):
             for d in range(2):
                 z_wait(i, 4, d)
@@ -263,7 +288,7 @@
             y_send(i, RV, RB, rv_r, RL, rl_r)
 
     def d_consume(p, t, lag):
-        @at_chunk(t, lag + 6)
+        @at_chunk(t, lag)
         def _(i):
             y_wait(i, RV, RB, rv_r)
             (consume_grad if p == 2 else consume_inner)(i)
@@ -296,8 +321,8 @@
         rows = pl.ds(pl.multiple_of((i % H) * W, W), W)
         IA[rows, :] += lax.dot_general(RV[i], AX[xs], (((0,), (0,)), ((), ())), preferred_element_type=F32)
 
-    def r_final(p, t):
-        @at_chunk(t, 6)
+    def r_final(p, t, lag):
+        @at_chunk(t, lag)
         def _(i):
             for d in range(2):
                 r_wait(i, 4, d)
@@ -323,32 +348,31 @@
                         XS.at[i], XR.at[i], x_s.at[i], x_r.at[i], dev(y, z, c, (x + i // H) % NX)
                     ).start()
 
-    def r_rings(t):
-        for k in (4, 3, 2):
-            @at_chunk(t, k + 1)
-            def _(i, k=k):
-                for d in range(2):
-                    r_wait(i, k - 1, d)
-                    mine = PF.at[i % NPF, zrow((z + NZ + SG[d] * (5 - k)) % NZ), :]
-                    if k == 2:
-                        half, rest = pl.ds(d * (W // 2), W // 2), pl.ds((1 - d) * (W // 2), W // 2)
-                        RSS[i, d, 1, :, rest] = mine[:, rest].astype(BF)
-                        RSS[i, d, 1, :, half] = (mine[:, half] + RSR[i, d, 0, :, half].astype(F32)).astype(BF)
-                    else:
-                        RSS[i, d, k - 1] = (mine[...] + RSR[i, d, k - 2].astype(F32)).astype(BF)
-                    r_send(i, k, d)
-
-    def r_relay(t):
-        @at_chunk(t, 1)
+    def r_ring(t, lag, k):
+        @at_chunk(t, lag)
+        def _(i):
+            for d in range(2):
+                r_wait(i, k - 1, d)
+                mine = PF.at[i % NPF, zrow((z + NZ + SG[d] * (5 - k)) % NZ), :]
+                if k == 2:
+                    half, rest = pl.ds(d * (W // 2), W // 2), pl.ds((1 - d) * (W // 2), W // 2)
+                    RSS[i, d, 1, :, rest] = mine[:, rest].astype(BF)
+                    RSS[i, d, 1, :, half] = (mine[:, half] + RSR[i, d, 0, :, half].astype(F32)).astype(BF)
+                else:
+                    RSS[i, d, k - 1] = (mine[...] + RSR[i, d, k - 2].astype(F32)).astype(BF)
+                r_send(i, k, d)
+
+    def r_relay(t, lag):
+        @at_chunk(t, lag)
         def _(i):
             y_relay(i, QV, T, qv_r, QL, ql_r, g_s)
 
-        @at_chunk(t, 3)
+        @at_chunk(t, lag + 2)
         def _(i):
             wait_send(QL.at[i], g_s.at[i])
 
-    def r_combine(t):
-        @at_chunk(t, 2)
+    def r_combine(t, lag):
+        @at_chunk(t, lag)
         def _(i):
             y_wait(i, QV, T, qv_r)
             PF[i % NPF] = jnp.dot(PT[...], QV[i], preferred_element_type=F32)
@@ -357,8 +381,8 @@
                 RSS[i, d, 0, :, ln] = PF[i % NPF, zrow((z + 4) % NZ), ln].astype(BF)
                 r_send(i, 1, d)
 
-    def r_piece(t):
-        @at_chunk(t, 0)
+    def r_piece(t, lag):
+        @at_chunk(t, lag)
         def _(i):
             YS[i] = lax.dot_general(
                 SC[...], UV[wide(col(i)), :], (((1,), (1,)), ((), ())), preferred_element_type=F32
@@ -377,56 +401,72 @@
             SC[rows, :] = (IA[rows, :] * SV[rows, :]).astype(BF)
             IA[rows, :] = jnp.zeros((128, HID), F32)
 
-    IA[...] = jnp.zeros_like(IA)
+    for copy in ins[:2]:
+        copy.wait()
+    tabulate()
+    ins[2].wait()
+
+    @pl.loop(0, NY)
+    def _(b):
+        activate(b)
+
+    TGR[x, z] = TV[z]
+    pl.semaphore_wait(barrier, NX * NZ - 1 + 2 * NC + 1)
 
     @pl.loop(0, NCH + 6)
     def _(t):
-        d_rings(0, t, 0)
+        for k in (4, 3, 2, 1):
+            d_ring(0, t, k - 1, k)
+
+        @pl.when(t == 0)
+        def _():
+            @pl.loop(1, NX * NZ)
+            def _(q):
+                xx = (x + q // NZ) % NX
+                zz = (z + q) % NZ
+                remote(TV.at[zz], TGR.at[x, z], tg_s.at[0], tg_r.at[x], dev(y, zz, c, xx)).start()
 
         @pl.when(t == 2)
         def _():
             wait_recv(TGR.at[x, pl.ds(0, NZ - 1)], tg_r.at[x])
+            build(x, True)
+
+        @pl.when(t == 4)
+        def _():
             for dx in range(1, NX):
                 xs = (x + dx) % NX
                 wait_recv(TGR.at[xs], tg_r.at[xs])
-            build(x, True)
-
-        @pl.when(t == 0)
-        def _():
-            ins[1].wait()
-
-        @pl.when(t < NY)
-        def _():
-            activate(t)
-
-        @pl.when(t == NY)
-        def _():
-            for copy in ins[2:]:
+            for copy in ins[3:]:
                 copy.wait()
             for dx in range(1, NX):
                 remote(AX.at[x], AX.at[x], ax_s.at[0], ax_r.at[x], dev(y, z, c, (x + dx) % NX)).start()
 
-        d_relay(0, t, 0)
-        d_select(0, t, 0)
-        d_consume(0, t, 0)
+        d_relay(0, t, 4)
+        d_select(0, t, 3)
+        d_consume(0, t, 6)
 
     d_sent()
 
     for p in (1, 2):
-        lag = 5 + p
+        lag = 4 + p
         scale_inner()
 
-        @pl.loop(0, NCH + 6 + lag)
+        @pl.loop(0, NCH + 5 + lag)
         def _(t, p=p, lag=lag):
-            r_final(p, t)
-            r_rings(t)
-            d_rings(p, t, lag)
-            r_relay(t)
-            d_relay(p, t, lag)
-            r_combine(t)
-            d_select(p, t, lag)
-            r_piece(t)
-            d_consume(p, t, lag)
+            r_relay(t, 1)
+            r_final(p, t, 5)
+            d_ring(p, t, lag + 3, 4)
+            d_ring(p, t, lag + 2, 3)
+            r_ring(t, 4, 4)
+            r_piece(t, 0)
+            d_consume(p, t, lag + 5)
+            d_ring(p, t, lag + 1, 2)
+            r_ring(t, 3, 3)
+            d_ring(p, t, lag, 1)
+            r_ring(t, 2, 2)
+            d_relay(p, t, lag + 4)
+            d_select(p, t, lag + 3)
+            r_combine(t, 1)
 
         r_sent()
         d_sent()
@@ -444,26 +484,16 @@
 
 
 def body(cotangent, expert_ids, gate_values, hidden_pre, up_weight, down_weight):
-    experts = NY * NZ * NC
-    onehot = expert_ids[:, :, None] == jnp.arange(experts, dtype=jnp.int32)[None, None, :]
-    named = jnp.any(onehot, axis=1)
-    count = named.astype(jnp.int32)
-    rank = jnp.cumsum(count, axis=0) - count
-    rank = jnp.where(named, rank, -1).astype(F32)
-    gate = jnp.sum(jnp.where(onehot, gate_values[:, :, None], 0.0), axis=1)
-
-    def planes(table):
-        return table.T.reshape(NY, NZ, NC, T).transpose(1, 0, 2, 3).reshape(NZ, NE, T)
-
-    tables = jnp.concatenate([planes(rank), planes(gate)], axis=1)
     vm, dma = pltpu.VMEM, pltpu.SemaphoreType.DMA
     input_grad, down_grad = pl.pallas_call(
         kernel,
         out_shape=(jax.ShapeDtypeStruct((T, D), BF), jax.ShapeDtypeStruct((H * W, HID), BF)),
-        in_specs=[pl.BlockSpec(memory_space=pl.ANY)] * 5,
+        in_specs=[pl.BlockSpec(memory_space=pl.ANY)] * 6,
         out_specs=(pl.BlockSpec(memory_space=pltpu.VMEM),) * 2,
         scratch_shapes=[
             vm((T, D), BF),
+            vm(expert_ids.shape[::-1], jnp.int32),
+            vm(gate_values.shape[::-1], F32),
             vm((NZ, 2 * NE, T), F32),
             vm((NX, NZ, 2 * NE, T), F32),
             vm((SL, HID), BF),
@@ -487,13 +517,13 @@
             vm((NCH, 2, 4, T, W), BF),
             vm((NCH, T, W), BF),
             vm((NCH, T, W), BF),
-            dma((NCH,)), dma((5,)), dma((1,)), dma((NX,)), dma((1,)), dma((NX,)),
+            dma((NCH,)), dma((6,)), dma((1,)), dma((NX,)), dma((1,)), dma((NX,)),
             dma((NCH,)), dma((2, 4, NCH)), dma((NCH,)), dma((2, NCH)), dma((NCH,)), dma((NCH,)), dma((NE, NCH)),
             dma((2, NCH)), dma((NE, NCH)), dma((NCH,)), dma((2, 4, NCH)), dma((NCH,)), dma((NCH,)),
         ],
-        compiler_params=pltpu.CompilerParams(has_side_effects=True, vmem_limit_bytes=67043328),
+        compiler_params=pltpu.CompilerParams(has_side_effects=True, collective_id=0, vmem_limit_bytes=67043328),
         name="layer",
-    )(cotangent, tables, hidden_pre[0], up_weight[0], down_weight[0])
+    )(cotangent, expert_ids.T, gate_values.T, hidden_pre[0], up_weight[0], down_weight[0])
     return (input_grad, down_grad[None])
 
 

time: 341 us -> 312 us (0.915)
  Pallas kernels: 333 us -> 305 us
    pallas_call x1, Pallas kernels: 333 us -> 305 us  [body(): pl.pallas_call(kernel, out_shape=(jax.ShapeDtypeStruct((T, D), BF), jax.S...]
where the time goes in v3:
time: 312 us; the launch traced here: 309 us
  Pallas kernels  305 us (98%)
  local copies, waits for them, and re-layouts  3.94 us (1%)
    pallas_call x1, Pallas kernels, body(): pl.pallas_call(kernel, out_shape=(jax.ShapeDtypeStruct((T, D), BF), jax.S...  305 us

profile of v3, /device:TPU:7, one launch (start us, length us, event | category | flops | bytes accessed | tf_op | source)
XLA Modules:
  0.0 309.2 jit_solution(18286687112139346012)
XLA Ops:
  0.6 304.6 %layer.1 = (bf16[128,2048]{1,0:T(8,128)(2,1)}, bf16[512,768]{1,0:T(8,128)(2,1)}) custom-call(bf16[128,2048]{1,0:T(8,128)(2,1)} %cot_hbm.1, s32[6,128]{1,0:T(8,128)} %bitcast.10, f32[6,128]{1,0:T(8,128)} %bitcast.11, bf16[896,768]{1,0:T(8,128)(2,1)} %bitcast.8, bf16[2048,768]{1,0:T(8,128)(2,1)} %bitcast.6, bf16[2048,768]{1,0:T(8,128)(2,1)} %bitcast.7), custom_call_target="tpu_custom_call" | custom-call | tf_op jit(solution)/shard_map/layer/pallas_call | solution.py:488
  305.3 1.9 copy.10
  307.2 2.1 copy.11

commit v4 on v3

--- a/solution.py
+++ b/solution.py
@@ -39,9 +39,9 @@
 def kernel(
     cot_hbm, id_hbm, gate_hbm, hid_hbm, up_hbm, down_hbm,
     ig_ref, dg_ref,
-    CV, IDV, GTV, TV, TGR, HV, SV, AX, UV, DV, PM, PT, G, ZB, YS, RL, RV, QL, QV, IA, SC, PF, RSS, RSR, XS, XR,
+    CV, IDV, GTV, TV, TGR, HV, SV, AX, UV, DV, PM, PT, G, ZB, YS, RV, QV, IA, SC, PF, RSS, RSR, XS, XR,
     l_zb, l_in, tg_s, tg_r, ax_s, ax_r,
-    z_s, z_r, y_s, rl_r, f_s, g_s, rv_r, ql_r, qv_r, rs_s, rs_r, x_s, x_r,
+    z_s, z_r, y_s, rv_r, qv_r, rs_s, rs_r, x_s, x_r,
 ):
     ex = lax.axis_index("expert")
     x = lax.axis_index("token")
@@ -88,6 +88,7 @@
         greet(dev(y, (z + q) % NZ, c, (x + q // NZ) % NX))
 
     for cc in range(NC):
+        greet(dev(y2, z, cc, x))
         greet(dev(yp, z, cc, x))
         greet(dev(ym, z, cc, x))
     greet(partner)
@@ -170,14 +171,14 @@
                     PT[s * T : (s + 1) * T, pl.ds(pl.multiple_of(o * T, T), T)] = hit.T.astype(BF)
             G[rows, :] = jnp.broadcast_to(gsum, (RB, 128))
 
-    def y_send(i, dst, pitch, rsem, relay, relay_r):
+    def y_send(i, dst, pitch, rsem):
         mine = dst.at[i, pl.ds(pl.multiple_of(me * pitch, 16), RB), :]
 
         def src(yy, cc):
             return YS.at[i, pl.ds(pl.multiple_of((yy * NC + cc) * RB, 16), RB), :]
 
-        remote(src(y2, 0), relay.at[i, 0], y_s.at[i], relay_r.at[0, i], dev(yp, z, c, x)).start()
-        remote(src(y2, 1), relay.at[i, 1], y_s.at[i], relay_r.at[1, i], dev(ym, z, c, x)).start()
+        for cc in range(NC):
+            remote(src(y2, cc), mine, y_s.at[i], rsem.at[me, i], dev(y2, z, cc, x)).start()
         for cc in range(NC):
             remote(src(yp, cc), mine, y_s.at[i], rsem.at[me, i], dev(yp, z, cc, x)).start()
             remote(src(ym, cc), mine, y_s.at[i], rsem.at[me, i], dev(ym, z, cc, x)).start()
@@ -186,18 +187,6 @@
             i, pl.ds(pl.multiple_of(me * RB, 16), RB), :
         ]
 
-    def y_relay(i, dst, pitch, rsem, relay, relay_r, fsem):
-        for d, (frm, to) in enumerate(((ym, yp), (yp, ym))):
-            o = frm * NC + c
-            wait_recv(relay.at[i, d], relay_r.at[d, i])
-            remote(
-                relay.at[i, d],
-                dst.at[i, pl.ds(pl.multiple_of(o * pitch, 16), RB), :],
-                fsem.at[i],
-                rsem.at[o, i],
-                dev(to, z, d, x),
-            ).start()
-
     def y_wait(i, dst, pitch, rsem):
         for q in range(1, NE):
             o = (me + q) % NE
@@ -205,35 +194,36 @@
 
     SG = (1, -1)
 
-    def lanes(k, d):
-        return pl.ds(d * (W // 2), W // 2) if k == 4 else pl.ds(0, W)
+    HT = T // 2
+
+    def z_ref(i, b, k, d):
+        rows = pl.ds(pl.multiple_of(b * T + d * HT, HT), HT) if k == 4 else zrow(b)
+        return ZB.at[i, rows, :]
 
     def z_send(i, k, d, src=None):
-        b = (z + NZ - SG[d] * (k - 1)) % NZ
-        ref = ZB.at[i, zrow(b), lanes(k, d)]
+        ref = z_ref(i, (z + NZ - SG[d] * (k - 1)) % NZ, k, d)
         remote(
             ref if src is None else src, ref, z_s.at[i], z_r.at[d, k - 1, i], dev(y, (z + NZ + SG[d]) % NZ, c, x)
         ).start()
 
     def z_wait(i, k, d):
-        b = (z + NZ - SG[d] * k) % NZ
-        wait_recv(ZB.at[i, zrow(b), lanes(k, d)], z_r.at[d, k - 1, i])
-
-    def r_lanes(k, d):
-        return pl.ds(d * (W // 2), W // 2) if k == 1 else pl.ds(0, W)
+        wait_recv(z_ref(i, (z + NZ - SG[d] * k) % NZ, k, d), z_r.at[d, k - 1, i])
+
+    def r_rows(k, d):
+        return pl.ds(d * HT, HT) if k == 1 else pl.ds(0, T)
 
     def r_send(i, k, d):
-        ln = r_lanes(k, d)
+        rows = r_rows(k, d)
         remote(
-            RSS.at[i, d, k - 1, :, ln],
-            RSR.at[i, d, k - 1, :, ln],
+            RSS.at[i, d, k - 1, rows, :],
+            RSR.at[i, d, k - 1, rows, :],
             rs_s.at[i],
             rs_r.at[d, k - 1, i],
             dev(y, (z + NZ + SG[d]) % NZ, c, x),
         ).start()
 
     def r_wait(i, k, d):
-        wait_recv(RSR.at[i, d, k - 1, :, r_lanes(k, d)], rs_r.at[d, k - 1, i])
+        wait_recv(RSR.at[i, d, k - 1, r_rows(k, d), :], rs_r.at[d, k - 1, i])
 
     def at_chunk(t, lag):
         i = t - lag
@@ -265,11 +255,6 @@
             if p == 2:
                 ZB[i, zme, :] = XR[i]
 
-    def d_relay(p, t, lag):
-        @at_chunk(t, lag)
-        def _(i):
-            y_relay(i, RV, RB, rv_r, RL, rl_r, f_s)
-
     def d_select(p, t, lag):
         @at_chunk(t, lag)
         def _(i):
@@ -285,7 +270,7 @@
             rows = jnp.dot(PM[...], ZB[i], preferred_element_type=F32)
             for n in range(W // 128):
                 YS[i, :, n * 128 : (n + 1) * 128] = (rows[:, n * 128 : (n + 1) * 128] * G[...]).astype(BF)
-            y_send(i, RV, RB, rv_r, RL, rl_r)
+            y_send(i, RV, RB, rv_r)
 
     def d_consume(p, t, lag):
         @at_chunk(t, lag)
@@ -300,7 +285,6 @@
         @pl.loop(0, NCH)
         def _(i):
             wait_send(ZB.at[i, pl.ds(0, (NZ - 1) * T), :], z_s.at[i])
-            wait_send(RL.at[i], f_s.at[i])
             y_sent(i)
 
     def consume_inner(i):
@@ -355,30 +339,21 @@
                 r_wait(i, k - 1, d)
                 mine = PF.at[i % NPF, zrow((z + NZ + SG[d] * (5 - k)) % NZ), :]
                 if k == 2:
-                    half, rest = pl.ds(d * (W // 2), W // 2), pl.ds((1 - d) * (W // 2), W // 2)
-                    RSS[i, d, 1, :, rest] = mine[:, rest].astype(BF)
-                    RSS[i, d, 1, :, half] = (mine[:, half] + RSR[i, d, 0, :, half].astype(F32)).astype(BF)
+                    half, rest = pl.ds(d * HT, HT), pl.ds((1 - d) * HT, HT)
+                    RSS[i, d, 1, rest, :] = mine[rest, :].astype(BF)
+                    RSS[i, d, 1, half, :] = (mine[half, :] + RSR[i, d, 0, half, :].astype(F32)).astype(BF)
                 else:
                     RSS[i, d, k - 1] = (mine[...] + RSR[i, d, k - 2].astype(F32)).astype(BF)
                 r_send(i, k, d)
 
-    def r_relay(t, lag):
-        @at_chunk(t, lag)
-        def _(i):
-            y_relay(i, QV, T, qv_r, QL, ql_r, g_s)
-
-        @at_chunk(t, lag + 2)
-        def _(i):
-            wait_send(QL.at[i], g_s.at[i])
-
     def r_combine(t, lag):
         @at_chunk(t, lag)
         def _(i):
             y_wait(i, QV, T, qv_r)
             PF[i % NPF] = jnp.dot(PT[...], QV[i], preferred_element_type=F32)
             for d in range(2):
-                ln = pl.ds(d * (W // 2), W // 2)
-                RSS[i, d, 0, :, ln] = PF[i % NPF, zrow((z + 4) % NZ), ln].astype(BF)
+                far = pl.ds(pl.multiple_of((z + 4) % NZ * T + d * HT, HT), HT)
+                RSS[i, d, 0, d * HT : (d + 1) * HT, :] = PF[i % NPF, far, :].astype(BF)
                 r_send(i, 1, d)
 
     def r_piece(t, lag):
@@ -387,7 +362,7 @@
             YS[i] = lax.dot_general(
                 SC[...], UV[wide(col(i)), :], (((1,), (1,)), ((), ())), preferred_element_type=F32
             ).astype(BF)
-            y_send(i, QV, T, qv_r, QL, ql_r)
+            y_send(i, QV, T, qv_r)
 
     def r_sent():
         @pl.loop(0, NCH)
@@ -411,9 +386,9 @@
         activate(b)
 
     TGR[x, z] = TV[z]
-    pl.semaphore_wait(barrier, NX * NZ - 1 + 2 * NC + 1)
-
-    @pl.loop(0, NCH + 6)
+    pl.semaphore_wait(barrier, NX * NZ - 1 + 3 * NC + 1)
+
+    @pl.loop(0, NCH + 4)
     def _(t):
         for k in (4, 3, 2, 1):
             d_ring(0, t, k - 1, k)
@@ -441,9 +416,8 @@
             for dx in range(1, NX):
                 remote(AX.at[x], AX.at[x], ax_s.at[0], ax_r.at[x], dev(y, z, c, (x + dx) % NX)).start()
 
-        d_relay(0, t, 4)
         d_select(0, t, 3)
-        d_consume(0, t, 6)
+        d_consume(0, t, 4)
 
     d_sent()
 
@@ -451,20 +425,18 @@
         lag = 4 + p
         scale_inner()
 
-        @pl.loop(0, NCH + 5 + lag)
+        @pl.loop(0, NCH + 4 + lag)
         def _(t, p=p, lag=lag):
-            r_relay(t, 1)
             r_final(p, t, 5)
             d_ring(p, t, lag + 3, 4)
             d_ring(p, t, lag + 2, 3)
             r_ring(t, 4, 4)
             r_piece(t, 0)
-            d_consume(p, t, lag + 5)
+            d_consume(p, t, lag + 4)
             d_ring(p, t, lag + 1, 2)
             r_ring(t, 3, 3)
             d_ring(p, t, lag, 1)
             r_ring(t, 2, 2)
-            d_relay(p, t, lag + 4)
             d_select(p, t, lag + 3)
             r_combine(t, 1)
 
@@ -481,6 +453,11 @@
         wait_send(AX.at[x], ax_s.at[0])
     wait_send(TGR.at[pl.ds(0, NX - 1)], tg_s.at[0])
     wait_send(TGR.at[x, pl.ds(0, NZ - 1)], tg_s.at[0])
+
+
+def hand_over(a_ref, b_ref, c_ref, d_ref):
+    c_ref[...] = a_ref[...]
+    d_ref[...] = b_ref[...]
 
 
 def body(cotangent, expert_ids, gate_values, hidden_pre, up_weight, down_weight):
@@ -506,9 +483,7 @@
             vm((SL, 128), F32),
             vm((NCH, ZR, W), BF),
             vm((NCH, SL, W), BF),
-            vm((NCH, 2, RB, W), BF),
             vm((NCH, SL, W), BF),
-            vm((NCH, 2, RB, W), BF),
             vm((NCH, NE * T, W), BF),
             vm((SL, HID), F32),
             vm((SL, HID), BF),
@@ -518,12 +493,19 @@
             vm((NCH, T, W), BF),
             vm((NCH, T, W), BF),
             dma((NCH,)), dma((6,)), dma((1,)), dma((NX,)), dma((1,)), dma((NX,)),
-            dma((NCH,)), dma((2, 4, NCH)), dma((NCH,)), dma((2, NCH)), dma((NCH,)), dma((NCH,)), dma((NE, NCH)),
-            dma((2, NCH)), dma((NE, NCH)), dma((NCH,)), dma((2, 4, NCH)), dma((NCH,)), dma((NCH,)),
+            dma((NCH,)), dma((2, 4, NCH)), dma((NCH,)), dma((NE, NCH)), dma((NE, NCH)),
+            dma((NCH,)), dma((2, 4, NCH)), dma((NCH,)), dma((NCH,)),
         ],
         compiler_params=pltpu.CompilerParams(has_side_effects=True, collective_id=0, vmem_limit_bytes=67043328),
         name="layer",
     )(cotangent, expert_ids.T, gate_values.T, hidden_pre[0], up_weight[0], down_weight[0])
+    input_grad, down_grad = pl.pallas_call(
+        hand_over,
+        out_shape=(jax.ShapeDtypeStruct((T, D), BF), jax.ShapeDtypeStruct((H * W, HID), BF)),
+        in_specs=[pl.BlockSpec(memory_space=pltpu.VMEM)] * 2,
+        out_specs=(pl.BlockSpec(memory_space=pltpu.VMEM),) * 2,
+        name="hand_over",
+    )(input_grad, down_grad)
     return (input_grad, down_grad[None])
 
 

time: 312 us -> 339 us (1.087)
  Pallas kernels: 305 us -> 335 us
  local copies, waits for them, and re-layouts: 3.94 us -> 0 us
    pallas_call x1, Pallas kernels: 305 us -> 333 us  [body(): pl.pallas_call(kernel, out_shape=(jax.ShapeDtypeStruct((T, D), BF), jax.S...]
    unnamed x2 -> x0, local copies, waits for them, and re-layouts: 3.94 us -> none
where the time goes in v4:
time: 339 us; the launch traced here: 336 us
  Pallas kernels  335 us (99%)
    pallas_call x1, Pallas kernels, body(): pl.pallas_call(kernel, out_shape=(jax.ShapeDtypeStruct((T, D), BF), jax.S...  333 us

profile of v4, /device:TPU:7, one launch (start us, length us, event | category | flops | bytes accessed | tf_op | source)
XLA Modules:
  0.0 336.1 jit_solution(12543466266843690960)
XLA Ops:
  0.6 333.1 %layer.1 = (bf16[128,2048]{1,0:T(8,128)(2,1)}, bf16[512,768]{1,0:T(8,128)(2,1)}) custom-call(bf16[128,2048]{1,0:T(8,128)(2,1)} %cot_hbm.1, s32[6,128]{1,0:T(8,128)} %bitcast.9, f32[6,128]{1,0:T(8,128)} %bitcast.10, bf16[896,768]{1,0:T(8,128)(2,1)} %bitcast.8, bf16[2048,768]{1,0:T(8,128)(2,1)} %bitcast.6, bf16[2048,768]{1,0:T(8,128)(2,1)} %bitcast.7), custom_call_target="tpu_custom_call" | custom-call | tf_op jit(solution)/shard_map/layer/pallas_call | solution.py:465
  333.7 2.4 hand_over.1

commit v5 on v4

--- a/solution.py
+++ b/solution.py
@@ -388,7 +388,7 @@
     TGR[x, z] = TV[z]
     pl.semaphore_wait(barrier, NX * NZ - 1 + 3 * NC + 1)
 
-    @pl.loop(0, NCH + 4)
+    @pl.loop(0, NCH + 6)
     def _(t):
         for k in (4, 3, 2, 1):
             d_ring(0, t, k - 1, k)
@@ -417,7 +417,7 @@
                 remote(AX.at[x], AX.at[x], ax_s.at[0], ax_r.at[x], dev(y, z, c, (x + dx) % NX)).start()
 
         d_select(0, t, 3)
-        d_consume(0, t, 4)
+        d_consume(0, t, 6)
 
     d_sent()
 
@@ -425,14 +425,14 @@
         lag = 4 + p
         scale_inner()
 
-        @pl.loop(0, NCH + 4 + lag)
+        @pl.loop(0, NCH + 7 + lag)
         def _(t, p=p, lag=lag):
             r_final(p, t, 5)
             d_ring(p, t, lag + 3, 4)
             d_ring(p, t, lag + 2, 3)
             r_ring(t, 4, 4)
             r_piece(t, 0)
-            d_consume(p, t, lag + 4)
+            d_consume(p, t, lag + 7)
             d_ring(p, t, lag + 1, 2)
             r_ring(t, 3, 3)
             d_ring(p, t, lag, 1)

time: 339 us -> 299 us (0.88)
  Pallas kernels: 335 us -> 296 us
    pallas_call x1, Pallas kernels: 333 us -> 293 us  [body(): pl.pallas_call(kernel, out_shape=(jax.ShapeDtypeStruct((T, D), BF), jax.S...]
where the time goes in v5:
time: 299 us; the launch traced here: 296 us
  Pallas kernels  296 us (99%)
    pallas_call x1, Pallas kernels, body(): pl.pallas_call(kernel, out_shape=(jax.ShapeDtypeStruct((T, D), BF), jax.S...  293 us

profile of v5, /device:TPU:7, one launch (start us, length us, event | category | flops | bytes accessed | tf_op | source)
XLA Modules:
  0.0 296.2 jit_solution(15384579632341939072)
XLA Ops:
  0.6 293.2 %layer.1 = (bf16[128,2048]{1,0:T(8,128)(2,1)}, bf16[512,768]{1,0:T(8,128)(2,1)}) custom-call(bf16[128,2048]{1,0:T(8,128)(2,1)} %cot_hbm.1, s32[6,128]{1,0:T(8,128)} %bitcast.9, f32[6,128]{1,0:T(8,128)} %bitcast.10, bf16[896,768]{1,0:T(8,128)(2,1)} %bitcast.8, bf16[2048,768]{1,0:T(8,128)(2,1)} %bitcast.6, bf16[2048,768]{1,0:T(8,128)(2,1)} %bitcast.7), custom_call_target="tpu_custom_call" | custom-call | tf_op jit(solution)/shard_map/layer/pallas_call | solution.py:465
  293.8 2.4 hand_over.1

commit v6 on v5

--- a/solution.py
+++ b/solution.py
@@ -260,10 +260,6 @@
         def _(i):
             for d in range(2):
                 z_wait(i, 4, d)
-            if p == 2:
-                @pl.when(i % H == 0)
-                def _():
-                    build((x + NX - i // H) % NX, False)
             if p > 0:
                 y_sent(i)
 
@@ -271,6 +267,10 @@
             for n in range(W // 128):
                 YS[i, :, n * 128 : (n + 1) * 128] = (rows[:, n * 128 : (n + 1) * 128] * G[...]).astype(BF)
             y_send(i, RV, RB, rv_r)
+            if p == 2:
+                @pl.when(((i + 1) % H == 0) & (i + 1 < NCH))
+                def _():
+                    build((x + NX - (i + 1) // H) % NX, False)
 
     def d_consume(p, t, lag):
         @at_chunk(t, lag)

time: 299 us -> 299 us (level)
  no operation moved by 1% of the time
where the time goes in v6:
time: 299 us; the launch traced here: 295 us
  Pallas kernels  295 us (99%)
    pallas_call x1, Pallas kernels, body(): pl.pallas_call(kernel, out_shape=(jax.ShapeDtypeStruct((T, D), BF), jax.S...  292 us

profile of v6, /device:TPU:7, one launch (start us, length us, event | category | flops | bytes accessed | tf_op | source)
XLA Modules:
  0.0 295.4 jit_solution(13547627473224166590)
XLA Ops:
  0.6 292.4 %layer.1 = (bf16[128,2048]{1,0:T(8,128)(2,1)}, bf16[512,768]{1,0:T(8,128)(2,1)}) custom-call(bf16[128,2048]{1,0:T(8,128)(2,1)} %cot_hbm.1, s32[6,128]{1,0:T(8,128)} %bitcast.9, f32[6,128]{1,0:T(8,128)} %bitcast.10, bf16[896,768]{1,0:T(8,128)(2,1)} %bitcast.8, bf16[2048,768]{1,0:T(8,128)(2,1)} %bitcast.6, bf16[2048,768]{1,0:T(8,128)(2,1)} %bitcast.7), custom_call_target="tpu_custom_call" | custom-call | tf_op jit(solution)/shard_map/layer/pallas_call | solution.py:465
  293.1 2.4 hand_over.1
